TPU v7x, 512 devices: a whole 4x4x16 slice. The times are simulated.
512 devices in a mesh: blk: 32 (over z, core), sub: 16 (over x, y).
Axes of the slice: x: 4, y: 4, z: 16, core: 2. Of those that a mesh axis runs over, the one named last changes fastest.
Arguments:
- rhs: float32 [4096, 16, 256], P(('blk', 'sub')), may hold values from -6 to 6
- leaf_neighbors: int32 [4096, 6], P(('blk', 'sub')), may hold values from -1 to 4095, as said below
- parent_neighbors: int32 [512, 6], replicated, may hold values from -1 to 511, as said below
- children: int32 [512, 8], replicated, may hold values from 0 to 4095, as said below
- owners: int32 [512], replicated, may hold values from 0 to 15, as said below
- parent_places: int32 [512], replicated, may hold values from 0 to 511, as said below
Outputs:
- leaf_solution: float32 [4096, 16, 256], P(('blk', 'sub'))
- parent_solution: float32 [1536, 16, 256], P(('blk', 'sub'))
Inputs may be any that keep to these rules, and one draw needn't show every extreme that they name: `leaf_neighbors`: entry f of block b is the leaf block across face f of b, or -1 on the domain's boundary; the relation is mutual. Leaves d * 8 onward are the blocks of device d in order of blk then sub; a range is the 128 leaves of one index of blk. The -x and +x neighbours of a leaf belong to the devices one index lower and one index higher along sub with the same blk index; its -y and +y neighbours belong to its own device; its -z and +z neighbours belong to its own device or to the device one index lower or higher along blk with the same sub index. `parent_neighbors`: entry f of parent p is the parent block across face f of p, or -1; mutual. Range r holds the parents r * 16 onward; x and y neighbours lie in the same range, -z and +z neighbours in the range just below or above. Entry o = 4 oz + 2 oy + ox names the child in octant (oz, oy, ox); every leaf is the child of one parent, and a parent's children lie in the leaf range with the same index as the parent's range; its four children with ox = 0 belong to one device of even index 2k along sub and its four with ox = 1 to the device 2k + 1 with the same blk index. `owners`: within each range no index owns more than 3 parents, and some index owns exactly 3. `parent_places`: A permutation; parents of range r have places r * 16 onward.
All inputs are finite; a program needn't handle non-finite values.
Results may differ from a plain program's by a relative error of at most 0.0003.
Values sent between devices are 32-bit elements; how exact they have to be, the bound alone decides.
A program may use at most 64 MiB of HBM per device.

v0:
```python
import jax
import jax.numpy as jnp
from jax import lax
from jax.sharding import PartitionSpec as P

ROOT_SWEEPS = 8
PMOST = 3


relax_weight = 0.8


def extended(block, sides, width):
    for axis, dim in sides:
        count = lax.axis_size(axis)
        forward = [(i, i + 1) for i in range(count - 1)]
        backward = [(target, source) for source, target in forward]
        low = lax.ppermute(
            lax.slice_in_dim(block, block.shape[dim] - width, None, axis=dim), axis, forward
        )
        high = lax.ppermute(lax.slice_in_dim(block, 0, width, axis=dim), axis, backward)
        block = jnp.concatenate([low, block, high], axis=dim)
    return block


def laid_out(pieces, dim):
    dims = list(pieces.shape[1:])
    dims[dim] *= pieces.shape[0]
    return jnp.moveaxis(pieces, 0, dim).reshape(dims)


def copy_for_each(array, axis):
    peers = lax.axis_size(axis)
    return lax.all_to_all(
        jnp.broadcast_to(array[None], (peers, *array.shape)), axis, 0, 0, tiled=True
    )


def gathered_copies(array, axis, dim):
    return laid_out(copy_for_each(array, axis), dim)


def lane_parts():
    lanes = jnp.arange(256, dtype=jnp.int32)
    return (lanes // 16, lanes % 16)


def exact_dot(left, table):
    return jnp.einsum("...k,kl->...l", left, table, precision=lax.Precision.HIGHEST)


def spread_table(column):
    lane_y, lane_x = lane_parts()
    picked = (jnp.arange(16, dtype=jnp.int32)[:, None] == lane_y[None, :]) & (
        lane_x[None, :] == column
    )
    return picked.astype(jnp.float32)


def block_faces(values):
    blocks = values.shape[0]
    stacked = jnp.stack(
        [
            values[:, :, 0::16].reshape(blocks, 256),
            values[:, :, 15::16].reshape(blocks, 256),
            values[:, :, 0:16].reshape(blocks, 256),
            values[:, :, 240:256].reshape(blocks, 256),
            values[:, 0],
            values[:, 15],
        ],
        axis=1,
    )
    return stacked


def apply_operator(values, ghosts):
    blocks = values.shape[0]
    lane_y, lane_x = lane_parts()
    ghost_x_low = ghosts[:, 0].reshape(blocks, 16, 16)
    ghost_x_high = ghosts[:, 1].reshape(blocks, 16, 16)
    ghost_y_low = ghosts[:, 2].reshape(blocks, 16, 16)
    ghost_y_high = ghosts[:, 3].reshape(blocks, 16, 16)
    from_left = jnp.where(
        lane_x[None, None, :] > 0, jnp.pad(values, ((0, 0), (0, 0), (1, 0)))[:, :, :256], 0.0
    )
    from_right = jnp.where(
        lane_x[None, None, :] < 15, jnp.pad(values, ((0, 0), (0, 0), (0, 1)))[:, :, 1:], 0.0
    )
    beside_all = from_left + exact_dot(ghost_x_low, spread_table(0))
    beside_all = beside_all + from_right + exact_dot(ghost_x_high, spread_table(15))
    beside_all = (
        beside_all
        + jnp.pad(values, ((0, 0), (0, 0), (16, 0)))[:, :, :256]
        + jnp.pad(ghost_y_low, ((0, 0), (0, 0), (0, 240)))
    )
    beside_all = (
        beside_all
        + jnp.pad(values, ((0, 0), (0, 0), (0, 16)))[:, :, 16:]
        + jnp.pad(ghost_y_high, ((0, 0), (0, 0), (240, 0)))
    )
    beside_all = beside_all + jnp.concatenate([ghosts[:, 4][:, None], values[:, :-1]], axis=1)
    beside_all = beside_all + jnp.concatenate([values[:, 1:], ghosts[:, 5][:, None]], axis=1)
    return 6.0 * values - beside_all


def jacobi_sweep(values, forcing, ghosts):
    return values + relax_weight / 6.0 * (forcing - apply_operator(values, ghosts))


def restrict_table():
    lane_y, lane_x = lane_parts()
    target = lane_y // 2 * 8 + lane_x // 2
    return (target[:, None] == jnp.arange(64, dtype=jnp.int32)[None, :]).astype(jnp.float32)


def coarse_table():
    lane_y, lane_x = lane_parts()
    target = lane_y // 4 * 4 + lane_x // 4
    return (target[:, None] == jnp.arange(16, dtype=jnp.int32)[None, :]).astype(jnp.float32)


def place_table():
    source_id = jnp.arange(256, dtype=jnp.int32)
    octant_y = source_id // 128
    octant_x = source_id // 64 % 2
    inner_y = source_id // 8 % 8
    inner_x = source_id % 8
    target = (8 * octant_y + inner_y) * 16 + 8 * octant_x + inner_x
    return (target[:, None] == jnp.arange(256, dtype=jnp.int32)[None, :]).astype(jnp.float32)


def restrict_octants(values):
    blocks = values.shape[0]
    paired = values.reshape(blocks, 8, 2, 256).sum(axis=2)
    return (exact_dot(paired, restrict_table()) * 0.5).reshape(blocks, 512)


def assemble(octant_rows):
    blocks = octant_rows.shape[0]
    arranged = (
        octant_rows.reshape(blocks, 2, 2, 2, 8, 64)
        .transpose(0, 1, 4, 2, 3, 5)
        .reshape(blocks, 16, 256)
    )
    return exact_dot(arranged, place_table())


def coarsen(values):
    blocks = values.shape[0]
    layered = values.reshape(blocks, 4, 4, 256).sum(axis=2)
    return (exact_dot(layered, coarse_table()) * 0.25).reshape(blocks, 64)


def widen_root(coarse):
    blocks = coarse.shape[0]
    flat = exact_dot(coarse.reshape(blocks, 4, 16), coarse_table().T)
    return jnp.repeat(flat, 4, axis=1)


def octant_split(values):
    blocks = values.shape[0]
    moved = exact_dot(values, place_table().T)
    return moved.reshape(blocks, 2, 8, 2, 2, 64).transpose(0, 1, 3, 4, 2, 5).reshape(blocks, 8, 512)


def widen_leaf(octant):
    blocks = octant.shape[0]
    flat = exact_dot(octant.reshape(blocks, 8, 64), restrict_table().T)
    return jnp.repeat(flat, 2, axis=1)


def slot_ranks(range_owners):
    width = range_owners.shape[1]
    same_owner = range_owners[:, :, None] == range_owners[:, None, :]
    earlier = (
        jnp.arange(width, dtype=jnp.int32)[:, None] > jnp.arange(width, dtype=jnp.int32)[None, :]
    )
    return jnp.sum(same_owner & earlier[None], axis=2)


def root_relax(root_values, root_source, row_len):
    plane_len = root_values.shape[1]
    padded_z = jnp.pad(root_values, ((1, 1), (0, 0)))
    padded_row = jnp.pad(root_values, ((0, 0), (row_len, row_len)))
    column_x = jnp.arange(plane_len, dtype=jnp.int32)[None, :] % row_len
    beside_all = padded_z[:-2] + padded_z[2:]
    beside_all = (
        beside_all
        + padded_row[:, :plane_len]
        + padded_row[:, 2 * row_len : 2 * row_len + plane_len]
    )
    beside_all = beside_all + jnp.where(
        column_x > 0, padded_row[:, row_len - 1 : row_len - 1 + plane_len], 0.0
    )
    beside_all = beside_all + jnp.where(
        column_x < row_len - 1, padded_row[:, row_len + 1 : row_len + 1 + plane_len], 0.0
    )
    return root_values + relax_weight / 6.0 * (root_source - (6.0 * root_values - beside_all))


def stack_table(range_faces, outer_faces):
    row_count = range_faces.shape[0]
    return jnp.concatenate(
        [
            range_faces.reshape(row_count * 6, 256),
            outer_faces[0],
            outer_faces[1],
            jnp.zeros((1, 256), jnp.float32),
        ],
        axis=0,
    )


def lookup(face_table, rows_index):
    blocks = rows_index.shape[0]
    return jnp.take(face_table, rows_index.reshape(-1), axis=0).reshape(blocks, 6, 256)


def table_index(neighbours, range_start, range_len):
    opposite = jnp.array([1, 0, 3, 2, 5, 4], dtype=jnp.int32)
    local_id = neighbours - range_start
    inside = (local_id >= 0) & (local_id < range_len)
    from_below = (neighbours >= 0) & (local_id < 0)
    from_above = local_id >= range_len
    rows_index = jnp.where(inside, local_id * 6 + opposite[None, :], range_len * 8)
    rows_index = jnp.where(from_below, range_len * 6 + local_id + range_len, rows_index)
    return jnp.where(from_above, range_len * 7 + local_id - range_len, rows_index)


def leaf_index(neighbours, blk_here, sub_here, sub_count):
    blocks = neighbours.shape[0]
    opposite = jnp.array([1, 0, 3, 2, 5, 4], dtype=jnp.int32)
    clamped = jnp.maximum(neighbours, 0)
    device_id = clamped // blocks
    local_id = clamped % blocks
    other_blk = device_id // sub_count
    other_sub = device_id % sub_count
    present = neighbours >= 0
    same_blk = present & (other_blk == blk_here)
    same_sub = present & (other_sub == sub_here)
    rows_index = jnp.where(same_blk & same_sub, local_id * 6 + opposite[None, :], blocks * 10)
    rows_index = jnp.where(
        same_blk & (other_sub == sub_here - 1), blocks * 6 + local_id, rows_index
    )
    rows_index = jnp.where(
        same_blk & (other_sub == sub_here + 1), blocks * 7 + local_id, rows_index
    )
    rows_index = jnp.where(
        same_sub & (other_blk == blk_here - 1), blocks * 8 + local_id, rows_index
    )
    rows_index = jnp.where(
        same_sub & (other_blk == blk_here + 1), blocks * 9 + local_id, rows_index
    )
    return rows_index


def leaf_table(values):
    face_rows = block_faces(values)
    blocks = face_rows.shape[0]
    side_rows = jnp.stack([face_rows[:, 0], face_rows[:, 1]], axis=0)
    side_wide = extended(side_rows, (("sub", 0),), 1)
    edge_rows = jnp.stack([face_rows[:, 4], face_rows[:, 5]], axis=0)
    edge_wide = extended(edge_rows, (("blk", 0),), 1)
    return jnp.concatenate(
        [
            face_rows.reshape(blocks * 6, 256),
            side_wide[0],
            side_wide[3],
            edge_wide[0],
            edge_wide[3],
            jnp.zeros((1, 256), jnp.float32),
        ],
        axis=0,
    )


def range_table(values):
    face_rows = block_faces(values)
    edge_rows = jnp.stack([face_rows[:, 4], face_rows[:, 5]], axis=0)
    widened = extended(edge_rows, (("blk", 0),), 1)
    return stack_table(face_rows, jnp.stack([widened[0], widened[3]], axis=0))


def local(rhs, leaf_neighbors, parent_neighbors, children, owners, parent_places):
    factor = relax_weight / 6.0
    blk_count = lax.axis_size("blk")
    sub_count = lax.axis_size("sub")
    blk_here = lax.axis_index("blk")
    sub_here = lax.axis_index("sub")
    blocks = rhs.shape[0]
    range_len = blocks * sub_count
    parent_len = range_len // 8
    range_start = blk_here * range_len
    parent_start = blk_here * parent_len
    leaf_rows = leaf_index(leaf_neighbors, blk_here, sub_here, sub_count)
    sweep_one = factor * rhs
    second = jacobi_sweep(sweep_one, rhs, lookup(leaf_table(sweep_one), leaf_rows))
    residual = rhs - apply_operator(second, lookup(leaf_table(second), leaf_rows))
    octant_rows = gathered_copies(restrict_octants(residual), "sub", 0)
    range_children = lax.dynamic_slice_in_dim(children, parent_start, parent_len, 0) - range_start
    ranks_all = slot_ranks(owners.reshape(blk_count, parent_len)).reshape(-1)
    range_owners = lax.dynamic_slice_in_dim(owners, parent_start, parent_len, 0)
    range_ranks = lax.dynamic_slice_in_dim(ranks_all, parent_start, parent_len, 0)
    slot_match = (range_owners[None, :] == sub_here) & (
        range_ranks[None, :] == jnp.arange(PMOST, dtype=jnp.int32)[:, None]
    )
    filled = jnp.any(slot_match, axis=1)
    slot_local = jnp.sum(
        jnp.where(slot_match, jnp.arange(parent_len, dtype=jnp.int32)[None, :], 0), axis=1
    )
    filled_gain = filled.astype(jnp.float32)[:, None, None]
    own_local = sub_here * blocks + jnp.arange(blocks, dtype=jnp.int32)
    matches = range_children.reshape(-1)[None, :] == own_local[:, None]
    flat_place = jnp.sum(
        jnp.where(matches, jnp.arange(parent_len * 8, dtype=jnp.int32)[None, :], 0), axis=1
    )
    leaf_parent = flat_place // 8
    leaf_octant = flat_place % 8
    source = assemble(octant_rows[range_children])
    parent_rows = table_index(
        lax.dynamic_slice_in_dim(parent_neighbors, parent_start, parent_len, 0),
        parent_start,
        parent_len,
    )
    global_places = lax.dynamic_slice_in_dim(parent_places, parent_start, parent_len, 0)
    keep_gain = jnp.ones((parent_len, 1, 1), jnp.float32)
    parent_one = factor * source
    parent_two = jacobi_sweep(parent_one, source, lookup(range_table(parent_one), parent_rows))
    parent_rest = source - apply_operator(parent_two, lookup(range_table(parent_two), parent_rows))
    coarse = coarsen(parent_rest)
    root_slab = (
        jnp.zeros((parent_len, 64), jnp.float32).at[global_places - parent_start].set(coarse)
    )
    ordered = gathered_copies(root_slab, "blk", 0)
    side_y = blocks // 4
    side_x = sub_count // 2
    root_source = (
        ordered.reshape(blk_count, side_y, side_x, 4, 4, 4)
        .transpose(0, 3, 1, 4, 2, 5)
        .reshape(4 * blk_count, 16 * side_y * side_x)
    )
    root_source = root_source - jnp.mean(root_source)
    root_values = jnp.zeros_like(root_source)
    for repeat in range(ROOT_SWEEPS):
        root_values = root_relax(root_values, root_source, 4 * side_x)
    root_back = (
        root_values.reshape(blk_count, 4, side_y, 4, side_x, 4)
        .transpose(0, 2, 4, 1, 3, 5)
        .reshape(blk_count * parent_len, 64)[global_places]
    )
    parent_three = parent_two + widen_root(root_back) * keep_gain
    parent_four = jacobi_sweep(parent_three, source, lookup(range_table(parent_three), parent_rows))
    parent_solution = parent_four[slot_local] * filled_gain
    own_parents = parent_four[leaf_parent]
    pieces = octant_split(own_parents)
    chosen = jnp.take_along_axis(pieces, leaf_octant[:, None, None], axis=1)[:, 0]
    leaf_three = second + widen_leaf(chosen)
    leaf_solution = jacobi_sweep(leaf_three, rhs, lookup(leaf_table(leaf_three), leaf_rows))
    return (leaf_solution, parent_solution)


def solution(mesh):
    in_specs = (P(("blk", "sub"), None, None), P(("blk", "sub"), None), P(), P(), P(), P())
    out_specs = (P(("blk", "sub"), None, None), P(("blk", "sub"), None, None))
    return jax.shard_map(local, mesh=mesh, in_specs=in_specs, out_specs=out_specs, check_vma=False)
```

profile of v0, /device:TPU:1, one launch (start us, length us, event | category | flops | bytes accessed | tf_op | source)
XLA Modules:
  0.0 181.8 jit_solution(1812689167157064864)
XLA Ops:
  0.6 1.0 broadcast_multiply_fusion.2
  2.1 4.0 %collective-permute-start = (f32[1,8,256]{2,1,0:T(8,128)S(1)}, f32[1,8,256]{2,1,0:T(8,128)S(1)}, u32[]{:S(2)}, u32[]{:S(2)}) collective-permute-start(f32[1,8,256]{2,1,0:T(8,128)S(1)} %stack_squeeze_stack_reshape.18), channel_id=1, source_target_pairs={{0,1},{1,2},{2,3},{3,4},{4,5},{5,6},{6,7},{7,8},{8,9},{9,10},{10,1... | collective-permute-start | bytes 24584 | tf_op jit(solution)/shard_map/ppermute | solution.py:18
  6.5 1.3 collective-permute-start.1
  7.8 4.4 %collective-permute-start.2 = (f32[1,8,256]{2,0,1:T(1,128)S(1)}, f32[1,8,256]{2,0,1:T(1,128)S(1)}, u32[]{:S(2)}, u32[]{:S(2)}) collective-permute-start(f32[1,8,256]{2,0,1:T(1,128)S(1)} %get-tuple-element.79), channel_id=1, source_target_pairs={{0,16},{16,32},{32,48},{48,64},{64,80},{80,96},{96,112},{112,128},... | collective-permute-start | bytes 24584 | tf_op jit(solution)/shard_map/ppermute | solution.py:18
  12.2 2.9 %collective-permute-start.3 = (f32[1,8,256]{2,0,1:T(1,128)S(1)}, f32[1,8,256]{2,0,1:T(1,128)S(1)}, u32[]{:S(2)}, u32[]{:S(2)}) collective-permute-start(f32[1,8,256]{2,0,1:T(1,128)S(1)} %get-tuple-element.78), channel_id=1, source_target_pairs={{16,0},{32,16},{48,32},{64,48},{80,64},{96,80},{112,96},{128,112},... | collective-permute-start | bytes 24584 | tf_op jit(solution)/shard_map/ppermute | solution.py:21
  15.5 0.7 select_select_fusion.1
  16.4 0.8 select_select_fusion
  17.4 0.8 dynamic-slice_compare_fusion
  18.1 0.8 eq.441
  19.9 0.8 compare_select_fusion
  20.8 0.8 compare_select_fusion.6
  22.2 0.6 gather_fusion.5
  23.5 1.1 fusion.60
  26.1 4.3 %collective-permute-start.4 = (f32[1,8,256]{2,1,0:T(8,128)S(1)}, f32[1,8,256]{2,1,0:T(8,128)S(1)}, u32[]{:S(2)}, u32[]{:S(2)}) collective-permute-start(f32[1,8,256]{2,1,0:T(8,128)S(1)} %stack_squeeze_stack_reshape.20), channel_id=1, source_target_pairs={{0,1},{1,2},{2,3},{3,4},{4,5},{5,6},{6,7},{7,8},{8,9},{9,10},{10,1... | collective-permute-start | bytes 24584 | tf_op jit(solution)/shard_map/ppermute | solution.py:18
  30.4 1.3 collective-permute-start.5
  31.7 2.9 %collective-permute-start.6 = (f32[1,8,256]{2,0,1:T(1,128)S(1)}, f32[1,8,256]{2,0,1:T(1,128)S(1)}, u32[]{:S(2)}, u32[]{:S(2)}) collective-permute-start(f32[1,8,256]{2,0,1:T(1,128)S(1)} %get-tuple-element.71), channel_id=1, source_target_pairs={{0,16},{16,32},{32,48},{48,64},{64,80},{80,96},{96,112},{112,128},... | collective-permute-start | bytes 24584 | tf_op jit(solution)/shard_map/ppermute | solution.py:18
  34.7 1.9 %collective-permute-start.7 = (f32[1,8,256]{2,0,1:T(1,128)S(1)}, f32[1,8,256]{2,0,1:T(1,128)S(1)}, u32[]{:S(2)}, u32[]{:S(2)}) collective-permute-start(f32[1,8,256]{2,0,1:T(1,128)S(1)} %get-tuple-element.70), channel_id=1, source_target_pairs={{16,0},{32,16},{48,32},{64,48},{80,64},{96,80},{112,96},{128,112},... | collective-permute-start | bytes 24584 | tf_op jit(solution)/shard_map/ppermute | solution.py:21
  36.7 3.0 %collective-permute-done.7 = f32[1,8,256]{2,0,1:T(1,128)S(1)} collective-permute-done((f32[1,8,256]{2,0,1:T(1,128)S(1)}, f32[1,8,256]{2,0,1:T(1,128)S(1)}, u32[]{:S(2)}, u32[]{:S(2)}) %collective-permute-start.7) | collective-permute-done | bytes 8224 | tf_op jit(solution)/shard_map/ppermute | solution.py:21
  39.7 0.6 gather_fusion.6
  41.8 0.7 broadcast_in_dim.364
  42.5 9.4 %all-to-all-start = ((f32[16,8,512]{2,1,0:T(8,128)}), f32[16,8,512]{2,1,0:T(8,128)S(1)}, u32[]{:S(2)}, u32[]{:S(2)}) async-start(f32[16,8,512]{2,1,0:T(8,128)} %broadcast_in_dim.364), calls=%async_computation | async-start | bytes 524288 | tf_op jit(solution)/shard_map/all_to_all | solution.py:34
  52.0 7.6 %all-to-all-done = f32[16,8,512]{2,1,0:T(8,128)S(1)} async-done(((f32[16,8,512]{2,1,0:T(8,128)}), f32[16,8,512]{2,1,0:T(8,128)S(1)}, u32[]{:S(2)}, u32[]{:S(2)}) %all-to-all-start) | async-done | bytes 262176 | tf_op jit(solution)/shard_map/all_to_all | solution.py:34
  59.5 0.8 gather_fusion
  60.7 0.5 reshape.485
  61.6 1.9 %collective-permute-start.9 = (f32[1,16,256]{2,0,1:T(1,128)S(1)}, f32[1,16,256]{2,0,1:T(1,128)S(1)}, u32[]{:S(2)}, u32[]{:S(2)}) collective-permute-start(f32[1,16,256]{2,0,1:T(1,128)S(1)} %get-tuple-element.49), channel_id=1, source_target_pairs={{16,0},{32,16},{48,32},{64,48},{80,64},{96,80},{112,96},{128,112},... | collective-permute-start | bytes 49160 | tf_op jit(solution)/shard_map/ppermute | solution.py:21
  63.6 3.6 %collective-permute-start.8 = (f32[1,16,256]{2,0,1:T(1,128)S(1)}, f32[1,16,256]{2,0,1:T(1,128)S(1)}, u32[]{:S(2)}, u32[]{:S(2)}) collective-permute-start(f32[1,16,256]{2,0,1:T(1,128)S(1)} %get-tuple-element.50), channel_id=1, source_target_pairs={{0,16},{16,32},{32,48},{48,64},{64,80},{80,96},{96,112},{112,128},... | collective-permute-start | bytes 49160 | tf_op jit(solution)/shard_map/ppermute | solution.py:18
  67.3 0.7 slice.505
  68.0 0.8 slice.506
  69.5 0.7 gather_fusion.7
  71.6 1.9 %collective-permute-start.11 = (f32[1,16,256]{2,0,1:T(1,128)S(1)}, f32[1,16,256]{2,0,1:T(1,128)S(1)}, u32[]{:S(2)}, u32[]{:S(2)}) collective-permute-start(f32[1,16,256]{2,0,1:T(1,128)S(1)} %get-tuple-element.41), channel_id=1, source_target_pairs={{16,0},{32,16},{48,32},{64,48},{80,64},{96,80},{112,96},{128,112},... | collective-permute-start | bytes 49160 | tf_op jit(solution)/shard_map/ppermute | solution.py:21
  73.6 3.6 %collective-permute-start.10 = (f32[1,16,256]{2,0,1:T(1,128)S(1)}, f32[1,16,256]{2,0,1:T(1,128)S(1)}, u32[]{:S(2)}, u32[]{:S(2)}) collective-permute-start(f32[1,16,256]{2,0,1:T(1,128)S(1)} %get-tuple-element.42), channel_id=1, source_target_pairs={{0,16},{16,32},{32,48},{48,64},{64,80},{80,96},{96,112},{112,128},... | collective-permute-start | bytes 49160 | tf_op jit(solution)/shard_map/ppermute | solution.py:18
  77.3 0.7 slice.523
  78.1 0.8 slice.524
  79.5 0.7 gather_fusion.8
  82.1 0.8 scatter_custom_fusion
  82.9 0.8 reshape.656
  83.8 20.3 %all-to-all-start.1 = ((f32[32,1,1024]{2,1,0:T(1,128)}), f32[32,1,1024]{2,1,0:T(1,128)S(1)}, u32[]{:S(2)}, u32[]{:S(2)}) async-start(f32[32,1,1024]{2,1,0:T(1,128)} %reshape.656), calls=%async_computation.1 | async-start | bytes 262144 | tf_op jit(solution)/shard_map/all_to_all | solution.py:34
  104.2 15.8 %all-to-all-done.1 = f32[32,1,1024]{2,1,0:T(1,128)S(1)} async-done(((f32[32,1,1024]{2,1,0:T(1,128)}), f32[32,1,1024]{2,1,0:T(1,128)S(1)}, u32[]{:S(2)}, u32[]{:S(2)}) %all-to-all-start.1) | async-done | bytes 131104 | tf_op jit(solution)/shard_map/all_to_all | solution.py:34
  120.0 0.5 broadcast.1102
  120.5 0.9 reduce.51
  121.8 0.7 reduce_sum.63
  123.2 4.6 %copy.60 = f32[32,4,2,4,8,4]{5,4,3,2,1,0:T(8,128)} copy(f32[32,4,2,4,8,4]{0,4,2,5,3,1:T(8,128)S(1)} %bitcast.148) | data formatting | bytes 262144 | tf_op jit(solution)/shard_map/sub | solution.py:342
  127.8 4.9 %sub.296 = f32[128,256]{1,0:T(8,128)S(1)} reshape(f32[32,4,2,4,8,4]{5,4,3,2,1,0:T(8,128)} %copy.60) | data formatting | bytes 262144 | tf_op jit(solution)/shard_map/sub | solution.py:342
  134.6 5.6 %reshape.493 = f32[32,4,2,4,8,4]{5,4,3,2,1,0:T(8,128)} reshape(f32[128,256]{1,0:T(8,128)S(1)} %fusion.135) | data formatting | bytes 262144 | tf_op jit(solution)/shard_map/reshape | solution.py:347
  140.3 9.7 %copy.61 = f32[32,2,8,4,4,4]{2,1,0,5,4,3:T(2,128)S(1)} copy(f32[32,2,8,4,4,4]{5,2,4,1,3,0:T(8,128)} %bitcast.147) | data formatting | bytes 262144 | tf_op jit(solution)/shard_map/transpose | solution.py:348
  150.0 3.2 %reshape.494 = f32[512,64]{0,1:T(8,128)S(1)} reshape(f32[32,2,8,4,4,4]{2,1,0,5,4,3:T(2,128)S(1)} %copy.61) | data formatting | bytes 262144 | tf_op jit(solution)/shard_map/reshape | solution.py:349
  153.3 0.6 gather_fusion.1
  154.4 3.5 %collective-permute-start.13 = (f32[1,16,256]{2,0,1:T(1,128)S(1)}, f32[1,16,256]{2,0,1:T(1,128)S(1)}, u32[]{:S(2)}, u32[]{:S(2)}) collective-permute-start(f32[1,16,256]{2,0,1:T(1,128)S(1)} %get-tuple-element.33), channel_id=1, source_target_pairs={{16,0},{32,16},{48,32},{64,48},{80,64},{96,80},{112,96},{128,112},... | collective-permute-start | bytes 49160 | tf_op jit(solution)/shard_map/ppermute | solution.py:21
  157.9 2.3 %collective-permute-start.12 = (f32[1,16,256]{2,0,1:T(1,128)S(1)}, f32[1,16,256]{2,0,1:T(1,128)S(1)}, u32[]{:S(2)}, u32[]{:S(2)}) collective-permute-start(f32[1,16,256]{2,0,1:T(1,128)S(1)} %get-tuple-element.34), channel_id=1, source_target_pairs={{0,16},{16,32},{32,48},{48,64},{64,80},{80,96},{96,112},{112,128},... | collective-permute-start | bytes 49160 | tf_op jit(solution)/shard_map/ppermute | solution.py:18
  160.3 0.7 slice.589
  161.1 0.8 slice.590
  162.5 0.7 gather_fusion.9
  164.6 0.6 gather_fusion.2
  165.1 0.4 fusion.69
  165.9 0.6 gather_fusion.4
  168.4 2.0 %collective-permute-start.14 = (f32[1,8,256]{2,1,0:T(8,128)S(1)}, f32[1,8,256]{2,1,0:T(8,128)S(1)}, u32[]{:S(2)}, u32[]{:S(2)}) collective-permute-start(f32[1,8,256]{2,1,0:T(8,128)S(1)} %stack_squeeze_stack_reshape.22), channel_id=1, source_target_pairs={{0,1},{1,2},{2,3},{3,4},{4,5},{5,6},{6,7},{7,8},{8,9},{9,10},{10,1... | collective-permute-start | bytes 24584 | tf_op jit(solution)/shard_map/ppermute | solution.py:18
  170.5 1.3 collective-permute-start.15
  171.8 2.8 %collective-permute-start.16 = (f32[1,8,256]{2,0,1:T(1,128)S(1)}, f32[1,8,256]{2,0,1:T(1,128)S(1)}, u32[]{:S(2)}, u32[]{:S(2)}) collective-permute-start(f32[1,8,256]{2,0,1:T(1,128)S(1)} %get-tuple-element.57), channel_id=1, source_target_pairs={{0,16},{16,32},{32,48},{48,64},{64,80},{80,96},{96,112},{112,128},... | collective-permute-start | bytes 24584 | tf_op jit(solution)/shard_map/ppermute | solution.py:18
  174.6 1.9 %collective-permute-start.17 = (f32[1,8,256]{2,0,1:T(1,128)S(1)}, f32[1,8,256]{2,0,1:T(1,128)S(1)}, u32[]{:S(2)}, u32[]{:S(2)}) collective-permute-start(f32[1,8,256]{2,0,1:T(1,128)S(1)} %get-tuple-element.56), channel_id=1, source_target_pairs={{16,0},{32,16},{48,32},{64,48},{80,64},{96,80},{112,96},{128,112},... | collective-permute-start | bytes 24584 | tf_op jit(solution)/shard_map/ppermute | solution.py:21
  176.5 0.6 gather_fusion.3
  177.1 0.7 broadcast_multiply_fusion.3
  177.8 1.7 collective-permute-done.17
  179.6 0.6 gather_fusion.10
  180.9 0.9 fusion.40
  (246 shorter events, 19.9 us)
Async XLA Ops:
  0.6 40.4 %copy-start = (f32[8,16,256]{2,1,0:T(8,128)S(1)}, f32[8,16,256]{2,1,0:T(8,128)}, u32[]{:S(2)}) copy-start(f32[8,16,256]{2,1,0:T(8,128)} %param.12) | copy-start | bytes 393220
  2.1 20.0 %collective-permute-start = (f32[1,8,256]{2,1,0:T(8,128)S(1)}, f32[1,8,256]{2,1,0:T(8,128)S(1)}, u32[]{:S(2)}, u32[]{:S(2)}) collective-permute-start(f32[1,8,256]{2,1,0:T(8,128)S(1)} %stack_squeeze_stack_reshape.18), channel_id=1, source_target_pairs={{0,1},{1,2},{2,3},{3,4},{4,5},{5,6},{6,7},{7,8},{8,9},{9,10},{10,1... | collective-permute-start | bytes 24584 | tf_op jit(solution)/shard_map/ppermute | solution.py:18
  6.5 15.5 %collective-permute-start.1 = (f32[1,8,256]{2,1,0:T(8,128)S(1)}, f32[1,8,256]{2,1,0:T(8,128)S(1)}, u32[]{:S(2)}, u32[]{:S(2)}) collective-permute-start(f32[1,8,256]{2,1,0:T(8,128)S(1)} %stack_squeeze_stack_reshape.19), channel_id=1, source_target_pairs={{1,0},{2,1},{3,2},{4,3},{5,4},{6,5},{7,6},{8,7},{9,8},{10,9},{11,1... | collective-permute-start | bytes 24584 | tf_op jit(solution)/shard_map/ppermute | solution.py:21
  7.8 14.2 %collective-permute-start.2 = (f32[1,8,256]{2,0,1:T(1,128)S(1)}, f32[1,8,256]{2,0,1:T(1,128)S(1)}, u32[]{:S(2)}, u32[]{:S(2)}) collective-permute-start(f32[1,8,256]{2,0,1:T(1,128)S(1)} %get-tuple-element.79), channel_id=1, source_target_pairs={{0,16},{16,32},{32,48},{48,64},{64,80},{80,96},{96,112},{112,128},... | collective-permute-start | bytes 24584 | tf_op jit(solution)/shard_map/ppermute | solution.py:18
  12.2 9.9 %collective-permute-start.3 = (f32[1,8,256]{2,0,1:T(1,128)S(1)}, f32[1,8,256]{2,0,1:T(1,128)S(1)}, u32[]{:S(2)}, u32[]{:S(2)}) collective-permute-start(f32[1,8,256]{2,0,1:T(1,128)S(1)} %get-tuple-element.78), channel_id=1, source_target_pairs={{16,0},{32,16},{48,32},{64,48},{80,64},{96,80},{112,96},{128,112},... | collective-permute-start | bytes 24584 | tf_op jit(solution)/shard_map/ppermute | solution.py:21
  26.1 10.5 %collective-permute-start.4 = (f32[1,8,256]{2,1,0:T(8,128)S(1)}, f32[1,8,256]{2,1,0:T(8,128)S(1)}, u32[]{:S(2)}, u32[]{:S(2)}) collective-permute-start(f32[1,8,256]{2,1,0:T(8,128)S(1)} %stack_squeeze_stack_reshape.20), channel_id=1, source_target_pairs={{0,1},{1,2},{2,3},{3,4},{4,5},{5,6},{6,7},{7,8},{8,9},{9,10},{10,1... | collective-permute-start | bytes 24584 | tf_op jit(solution)/shard_map/ppermute | solution.py:18
  30.4 6.2 %collective-permute-start.5 = (f32[1,8,256]{2,1,0:T(8,128)S(1)}, f32[1,8,256]{2,1,0:T(8,128)S(1)}, u32[]{:S(2)}, u32[]{:S(2)}) collective-permute-start(f32[1,8,256]{2,1,0:T(8,128)S(1)} %stack_squeeze_stack_reshape.21), channel_id=1, source_target_pairs={{1,0},{2,1},{3,2},{4,3},{5,4},{6,5},{7,6},{8,7},{9,8},{10,9},{11,1... | collective-permute-start | bytes 24584 | tf_op jit(solution)/shard_map/ppermute | solution.py:21
  31.7 4.9 %collective-permute-start.6 = (f32[1,8,256]{2,0,1:T(1,128)S(1)}, f32[1,8,256]{2,0,1:T(1,128)S(1)}, u32[]{:S(2)}, u32[]{:S(2)}) collective-permute-start(f32[1,8,256]{2,0,1:T(1,128)S(1)} %get-tuple-element.71), channel_id=1, source_target_pairs={{0,16},{16,32},{32,48},{48,64},{64,80},{80,96},{96,112},{112,128},... | collective-permute-start | bytes 24584 | tf_op jit(solution)/shard_map/ppermute | solution.py:18
  34.7 5.0 %collective-permute-start.7 = (f32[1,8,256]{2,0,1:T(1,128)S(1)}, f32[1,8,256]{2,0,1:T(1,128)S(1)}, u32[]{:S(2)}, u32[]{:S(2)}) collective-permute-start(f32[1,8,256]{2,0,1:T(1,128)S(1)} %get-tuple-element.70), channel_id=1, source_target_pairs={{16,0},{32,16},{48,32},{64,48},{80,64},{96,80},{112,96},{128,112},... | collective-permute-start | bytes 24584 | tf_op jit(solution)/shard_map/ppermute | solution.py:21
  42.5 17.0 %all-to-all-start = ((f32[16,8,512]{2,1,0:T(8,128)}), f32[16,8,512]{2,1,0:T(8,128)S(1)}, u32[]{:S(2)}, u32[]{:S(2)}) async-start(f32[16,8,512]{2,1,0:T(8,128)} %broadcast_in_dim.364), calls=%async_computation | async-start | bytes 524288 | tf_op jit(solution)/shard_map/all_to_all | solution.py:34
  61.6 7.8 %collective-permute-start.9 = (f32[1,16,256]{2,0,1:T(1,128)S(1)}, f32[1,16,256]{2,0,1:T(1,128)S(1)}, u32[]{:S(2)}, u32[]{:S(2)}) collective-permute-start(f32[1,16,256]{2,0,1:T(1,128)S(1)} %get-tuple-element.49), channel_id=1, source_target_pairs={{16,0},{32,16},{48,32},{64,48},{80,64},{96,80},{112,96},{128,112},... | collective-permute-start | bytes 49160 | tf_op jit(solution)/shard_map/ppermute | solution.py:21
  63.6 5.9 %collective-permute-start.8 = (f32[1,16,256]{2,0,1:T(1,128)S(1)}, f32[1,16,256]{2,0,1:T(1,128)S(1)}, u32[]{:S(2)}, u32[]{:S(2)}) collective-permute-start(f32[1,16,256]{2,0,1:T(1,128)S(1)} %get-tuple-element.50), channel_id=1, source_target_pairs={{0,16},{16,32},{32,48},{48,64},{64,80},{80,96},{96,112},{112,128},... | collective-permute-start | bytes 49160 | tf_op jit(solution)/shard_map/ppermute | solution.py:18
  71.6 7.8 %collective-permute-start.11 = (f32[1,16,256]{2,0,1:T(1,128)S(1)}, f32[1,16,256]{2,0,1:T(1,128)S(1)}, u32[]{:S(2)}, u32[]{:S(2)}) collective-permute-start(f32[1,16,256]{2,0,1:T(1,128)S(1)} %get-tuple-element.41), channel_id=1, source_target_pairs={{16,0},{32,16},{48,32},{64,48},{80,64},{96,80},{112,96},{128,112},... | collective-permute-start | bytes 49160 | tf_op jit(solution)/shard_map/ppermute | solution.py:21
  73.6 5.9 %collective-permute-start.10 = (f32[1,16,256]{2,0,1:T(1,128)S(1)}, f32[1,16,256]{2,0,1:T(1,128)S(1)}, u32[]{:S(2)}, u32[]{:S(2)}) collective-permute-start(f32[1,16,256]{2,0,1:T(1,128)S(1)} %get-tuple-element.42), channel_id=1, source_target_pairs={{0,16},{16,32},{32,48},{48,64},{64,80},{80,96},{96,112},{112,128},... | collective-permute-start | bytes 49160 | tf_op jit(solution)/shard_map/ppermute | solution.py:18
  83.8 36.2 %all-to-all-start.1 = ((f32[32,1,1024]{2,1,0:T(1,128)}), f32[32,1,1024]{2,1,0:T(1,128)S(1)}, u32[]{:S(2)}, u32[]{:S(2)}) async-start(f32[32,1,1024]{2,1,0:T(1,128)} %reshape.656), calls=%async_computation.1 | async-start | bytes 262144 | tf_op jit(solution)/shard_map/all_to_all | solution.py:34
  154.4 8.0 %collective-permute-start.13 = (f32[1,16,256]{2,0,1:T(1,128)S(1)}, f32[1,16,256]{2,0,1:T(1,128)S(1)}, u32[]{:S(2)}, u32[]{:S(2)}) collective-permute-start(f32[1,16,256]{2,0,1:T(1,128)S(1)} %get-tuple-element.33), channel_id=1, source_target_pairs={{16,0},{32,16},{48,32},{64,48},{80,64},{96,80},{112,96},{128,112},... | collective-permute-start | bytes 49160 | tf_op jit(solution)/shard_map/ppermute | solution.py:21
  157.9 4.6 %collective-permute-start.12 = (f32[1,16,256]{2,0,1:T(1,128)S(1)}, f32[1,16,256]{2,0,1:T(1,128)S(1)}, u32[]{:S(2)}, u32[]{:S(2)}) collective-permute-start(f32[1,16,256]{2,0,1:T(1,128)S(1)} %get-tuple-element.34), channel_id=1, source_target_pairs={{0,16},{16,32},{32,48},{48,64},{64,80},{80,96},{96,112},{112,128},... | collective-permute-start | bytes 49160 | tf_op jit(solution)/shard_map/ppermute | solution.py:18
  168.4 9.4 %collective-permute-start.14 = (f32[1,8,256]{2,1,0:T(8,128)S(1)}, f32[1,8,256]{2,1,0:T(8,128)S(1)}, u32[]{:S(2)}, u32[]{:S(2)}) collective-permute-start(f32[1,8,256]{2,1,0:T(8,128)S(1)} %stack_squeeze_stack_reshape.22), channel_id=1, source_target_pairs={{0,1},{1,2},{2,3},{3,4},{4,5},{5,6},{6,7},{7,8},{8,9},{9,10},{10,1... | collective-permute-start | bytes 24584 | tf_op jit(solution)/shard_map/ppermute | solution.py:18
  170.5 7.3 %collective-permute-start.15 = (f32[1,8,256]{2,1,0:T(8,128)S(1)}, f32[1,8,256]{2,1,0:T(8,128)S(1)}, u32[]{:S(2)}, u32[]{:S(2)}) collective-permute-start(f32[1,8,256]{2,1,0:T(8,128)S(1)} %stack_squeeze_stack_reshape.23), channel_id=1, source_target_pairs={{1,0},{2,1},{3,2},{4,3},{5,4},{6,5},{7,6},{8,7},{9,8},{10,9},{11,1... | collective-permute-start | bytes 24584 | tf_op jit(solution)/shard_map/ppermute | solution.py:21
  171.8 6.0 %collective-permute-start.16 = (f32[1,8,256]{2,0,1:T(1,128)S(1)}, f32[1,8,256]{2,0,1:T(1,128)S(1)}, u32[]{:S(2)}, u32[]{:S(2)}) collective-permute-start(f32[1,8,256]{2,0,1:T(1,128)S(1)} %get-tuple-element.57), channel_id=1, source_target_pairs={{0,16},{16,32},{32,48},{48,64},{64,80},{80,96},{96,112},{112,128},... | collective-permute-start | bytes 24584 | tf_op jit(solution)/shard_map/ppermute | solution.py:18
  174.6 5.0 %collective-permute-start.17 = (f32[1,8,256]{2,0,1:T(1,128)S(1)}, f32[1,8,256]{2,0,1:T(1,128)S(1)}, u32[]{:S(2)}, u32[]{:S(2)}) collective-permute-start(f32[1,8,256]{2,0,1:T(1,128)S(1)} %get-tuple-element.56), channel_id=1, source_target_pairs={{16,0},{32,16},{48,32},{64,48},{80,64},{96,80},{112,96},{128,112},... | collective-permute-start | bytes 24584 | tf_op jit(solution)/shard_map/ppermute | solution.py:21
where the time goes:
time: 185 us; the launch traced here: 182 us
  starting transfers between devices  77.8 us (42%)
  local copies, waits for them, and re-layouts  56.2 us (30%)
  waiting for transfers between devices  28.1 us (15%)
  other arithmetic  10.5 us (6%)
  matrix products  6.12 us (3%)
  between operations  3.06 us (2%)
    ppermute x9, starting transfers between devices, extended(): lax.ppermute(lax.slice_in_dim(block, block.shape[dim] - width, None, axis...  30 us
    all_to_all x2, starting transfers between devices, copy_for_each(): lax.all_to_all(jnp.broadcast_to(array[None], (peers, *array.shape)), axis...  29.8 us
    all_to_all x2, waiting for transfers between devices, copy_for_each(): lax.all_to_all(jnp.broadcast_to(array[None], (peers, *array.shape)), axis...  23.4 us
    ppermute x9, starting transfers between devices, extended(): lax.ppermute(lax.slice_in_dim(block, 0, width, axis=dim), axis, backward)  18 us
    transpose x1, local copies, waits for them, and re-layouts, local(): root_back = root_values.reshape(blk_count, 4, side_y, 4, side_x, 4).trans...  9.71 us
    sub x2, local copies, waits for them, and re-layouts, local(): root_source = root_source - jnp.mean(root_source)  9.55 us
    dot_general x18, matrix products, exact_dot(): jnp.einsum('...k,kl->...l', left, table, precision=lax.Precision.HIGHEST)  6.12 us
    reshape x1, local copies, waits for them, and re-layouts, local(): root_values.reshape(blk_count, 4, side_y, 4, side_x, 4)  5.64 us
  transfers between devices with their start and end apart: 20, of which 4 were waited for; matrix products, arithmetic and copies ran while one was open for 8% of the time, Pallas kernels for 0%

commit v1 on v0

v1 whole, which is shorter than its diff:
```python
import jax
import jax.numpy as jnp
from jax import lax
from jax.experimental import pallas as pl
from jax.experimental.pallas import tpu as pltpu
from jax.sharding import PartitionSpec as P

FACTOR = 0.8 / 6.0
SWEEPS = 8
MESH = pl.DeviceIdType.MESH
LEAVES_HERE = 8
PARENTS_HERE = 16


def lane_roll(half, shift):
    return pltpu.roll(half, shift % 128, 1)


def row_roll(half, shift):
    return pltpu.roll(half, shift % half.shape[0], 0)


def both(ref, index):
    return [ref[0, index], ref[1, index]]


def lanes_of(ref, index):
    return [ref[index, :, 0:128], ref[index, :, 128:256]]


def flat_pair(ref, rows):
    return [ref[rows, 0:128], ref[rows, 128:256]]


def row_pair(ref, index):
    return [ref[index, :, 0:128], ref[index, :, 128:256]]


def put_row(ref, index, pair):
    ref[index, :, 0:128] = pair[0]
    ref[index, :, 128:256] = pair[1]


def put(ref, index, pair):
    ref[0, index] = pair[0]
    ref[1, index] = pair[1]


def put_flat(ref, rows, pair):
    ref[rows, 0:128] = pair[0]
    ref[rows, 128:256] = pair[1]


def split_dot(left, table):
    high = left.astype(jnp.bfloat16)
    low = (left - high.astype(jnp.float32)).astype(jnp.bfloat16)
    return jnp.dot(high, table, preferred_element_type=jnp.float32) + jnp.dot(
        low, table, preferred_element_type=jnp.float32
    )


def y_sum(lane, h, below, above):
    up = [lane_roll(h[0], 16), lane_roll(h[1], 16)]
    down = [lane_roll(h[0], -16), lane_roll(h[1], -16)]
    first = jnp.where(lane < 16, lane_roll(below, 16), up[0]) + jnp.where(
        lane >= 112, down[1], down[0]
    )
    second = jnp.where(lane < 16, up[0], up[1]) + jnp.where(
        lane >= 112, lane_roll(above, -16), down[1]
    )
    return [first, second]


def x_sum(lane, h, low, high):
    column = lane % 16
    return [
        jnp.where(column == 0, low[i], lane_roll(h[i], 1))
        + jnp.where(column == 15, high[i], lane_roll(h[i], -1))
        for i in range(2)
    ]


def z_sum(row, h, low, high):
    return [
        jnp.where(row == 0, low[i], row_roll(h[i], 1))
        + jnp.where(row == 15, high[i], row_roll(h[i], -1))
        for i in range(2)
    ]


def kernel(
    rhs,
    ln,
    pn,
    ch,
    ow,
    places,
    chv,
    leaf_out,
    parent_out,
    lv1,
    lv2,
    lv3,
    xs1,
    xs2,
    xs3,
    xr1,
    xr2,
    xr3,
    xt,
    zb1,
    zb2,
    zb3,
    res,
    oct_rows,
    src,
    pv1,
    pv2,
    pv3,
    pv4,
    geo,
    hsend,
    hrecv,
    hv,
    h2,
    own_rows,
    halo_two,
    rows_tmp,
    zq,
    slab,
    rbuf,
    rw,
    wm,
    we,
    msend,
    mrecv,
    lw,
    a_send,
    a_recv,
    c_send,
    c_recv,
    d_send,
    d_recv,
    f_send,
    f_recv,
    m_send,
    m_recv,
    tok,
):
    ranges = lax.axis_size("blk")
    subs = lax.axis_size("sub")
    r = lax.axis_index("blk")
    s = lax.axis_index("sub")
    barrier = pltpu.get_barrier_semaphore()
    for k in range(1, 16):
        pl.semaphore_signal(barrier, inc=1, device_id=(r, (s + k) % subs), device_id_type=MESH)
    for d in (1, -1, 2, -2):
        pl.semaphore_signal(
            barrier, inc=1, device_id=((r + d + ranges) % ranges, s), device_id_type=MESH
        )

    lane = lax.broadcasted_iota(jnp.int32, (16, 128), 1)
    row = lax.broadcasted_iota(jnp.int32, (16, 128), 0)
    column = lane % 16
    column8 = column[0:8]
    zero_half = jnp.zeros((16, 128), jnp.float32)
    zeros = [zero_half, zero_half]

    here = r * subs + s
    leaf_y = [[None, None] for _ in range(LEAVES_HERE)]
    leaf_x = [[None, None] for _ in range(LEAVES_HERE)]
    leaf_z = [[None, None] for _ in range(LEAVES_HERE)]
    for b in range(LEAVES_HERE):
        for f in range(6):
            n = ln[b, f]
            local = jnp.where(n >= 0, n & 7, 8)
            if f < 2:
                leaf_x[b][f] = local
            elif f < 4:
                leaf_y[b][f - 2] = local
            else:
                remote = (n >> 3) != here
                own_base, far_base = (8, 16) if f == 4 else (0, 24)
                leaf_z[b][f - 4] = jnp.where(
                    n >= 0, (n & 7) + jnp.where(remote, far_base, own_base), 32
                )

    def pack_faces(values, xs, zb):
        for h in range(2):
            low = jnp.zeros((8, 128), jnp.float32)
            high = jnp.zeros((8, 128), jnp.float32)
            for b in range(LEAVES_HERE):
                for part in range(2):
                    v = values[h, b, part * 8 : part * 8 + 8, :]
                    k = part * 8 + b
                    low = jnp.where(column8 == k, lane_roll(v, k), low)
                    high = jnp.where(column8 == k, lane_roll(v, k - 15), high)
            xs[0, :, h * 128 : h * 128 + 128] = low
            xs[1, :, h * 128 : h * 128 + 128] = high
        for b in range(LEAVES_HERE):
            put_row(zb, b, [values[i, b, 0:1, :] for i in range(2)])
            put_row(zb, 8 + b, [values[i, b, 15:16, :] for i in range(2)])
        zb[32] = jnp.zeros((1, 256), jnp.float32)

    def exchange(step, xs, xr, zb):
        def remote(source, target, slot, device):
            return pltpu.make_async_remote_copy(
                src_ref=source,
                dst_ref=target,
                send_sem=a_send.at[step, slot],
                recv_sem=a_recv.at[step, slot],
                device_id=device,
                device_id_type=MESH,
            )

        return (
            (s > 0, s < subs - 1, remote(xs.at[0], xr.at[1], 0, (r, (s + subs - 1) % subs))),
            (s < subs - 1, s > 0, remote(xs.at[1], xr.at[0], 1, (r, (s + 1) % subs))),
            (
                r > 0,
                r < ranges - 1,
                remote(zb.at[0:8], zb.at[24:32], 2, ((r + ranges - 1) % ranges, s)),
            ),
            (
                r < ranges - 1,
                r > 0,
                remote(zb.at[8:16], zb.at[16:24], 3, ((r + 1) % ranges, s)),
            ),
        )

    def start_all(copies):
        for sends, _, copy in copies:

            @pl.when(sends)
            def _():
                copy.start()

    def wait_arrivals(copies):
        for _, arrives, copy in copies:

            @pl.when(arrives)
            def _():
                copy.wait_recv()

    def wait_departures(copies):
        for sends, _, copy in copies:

            @pl.when(sends)
            def _():
                copy.wait_send()

    def unpack_x(xr):
        for h in range(2):
            lanes = slice(h * 128, h * 128 + 128)
            below = xr[0, :, lanes]
            above = xr[1, :, lanes]
            for j in range(LEAVES_HERE):
                for part in range(2):
                    k = part * 8 + j
                    rows = slice(part * 8, part * 8 + 8)
                    xt[0, h, j, rows, :] = lane_roll(below, -k)
                    xt[1, h, j, rows, :] = lane_roll(above, 15 - k)

    def leaf_beside(values, zb, b):
        h = both(values, b)
        low = [xt[0, i, leaf_x[b][0]] for i in range(2)]
        high = [xt[1, i, leaf_x[b][1]] for i in range(2)]
        xsum = x_sum(lane, h, low, high)
        ysum = y_sum(
            lane,
            h,
            values[1, leaf_y[b][0]],
            values[0, leaf_y[b][1]],
        )
        zsum = z_sum(
            row,
            h,
            row_pair(zb, leaf_z[b][0]),
            row_pair(zb, leaf_z[b][1]),
        )
        return h, [xsum[i] + ysum[i] + zsum[i] for i in range(2)]

    def relaxed(h, beside, forcing):
        return [h[i] + FACTOR * (forcing[i] - (6.0 * h[i] - beside[i])) for i in range(2)]

    def rest(h, beside, forcing):
        return [forcing[i] - (6.0 * h[i] - beside[i]) for i in range(2)]

    for ref in (lv1, lv2, lv3):
        put(ref, 8, zeros)
    for ref in (pv1, pv2, pv3):
        put(ref, 16, zeros)
    for side in range(2):
        xt[side, 0, 8] = zero_half
        xt[side, 1, 8] = zero_half
    for side in range(2):
        for ref in (hv, h2, own_rows):
            ref[side * 17 + 16] = jnp.zeros((1, 256), jnp.float32)

    for b in range(LEAVES_HERE):
        put(lv1, b, [FACTOR * v for v in lanes_of(rhs, b)])
    pack_faces(lv1, xs1, zb1)
    pl.semaphore_wait(barrier, 19)
    first = exchange(0, xs1, xr1, zb1)
    start_all(first)

    def greet(step, distance):
        for d in (distance, -distance):
            pl.semaphore_signal(
                tok.at[step],
                inc=1,
                device_id=((r + d + ranges) % ranges, s),
                device_id_type=MESH,
            )

    greet(0, 2)

    def numbers(shape, dim):
        return lax.broadcasted_iota(jnp.int32, shape, dim)

    def table(hit):
        return jnp.where(hit, 1.0, 0.0).astype(jnp.bfloat16)

    source_id = numbers((512, 128), 0)
    target_id = numbers((512, 128), 1)
    restrict = table(
        ((source_id % 256) // 32 == target_id // 16)
        & ((source_id % 16) // 2 + (source_id // 256) * 8 == target_id % 16)
    )
    fine = numbers((256, 256), 0)
    grid = numbers((256, 256), 1)
    coarse_table = table(
        (fine // 64 == (grid // 32) % 4) & ((fine % 16) // 4 == grid % 4)
    )
    grid_in = numbers((256, 256), 0)
    fine_out = numbers((256, 256), 1)
    widen_table = table(
        (fine_out // 64 == (grid_in // 32) % 4) & ((fine_out % 16) // 4 == grid_in % 4)
    )
    octant_in = numbers((128, 256), 0)
    leaf_cell = numbers((128, 256), 1)
    leaf_table = table(
        (octant_in // 16 == leaf_cell // 32)
        & (octant_in % 16 == (leaf_cell % 16) // 2 + (s % 2) * 8)
    )

    def inside(n, base):
        return jnp.where(n >= 0, jnp.clip(n - base, 0, 15), 16)

    mine = r * 16
    lower = jnp.maximum(r - 1, 0) * 16
    upper = jnp.minimum(r + 1, ranges - 1) * 16
    own_ghost = [
        [
            inside(pn[f, mine + p], mine if f < 4 else (lower if f == 4 else upper))
            for f in range(6)
        ]
        for p in range(PARENTS_HERE)
    ]
    halo_base = (lower, upper)
    halo_ghost = [
        [[inside(pn[f, base + q], base) for f in range(4)] for q in range(PARENTS_HERE)]
        for base in halo_base
    ]
    halo_own = [
        [
            inside(pn[5 - side, halo_base[side] + q], mine)
            for q in range(PARENTS_HERE)
        ]
        for side in range(2)
    ]

    wait_arrivals(first)
    unpack_x(xr1)
    for b in range(LEAVES_HERE):
        h, beside = leaf_beside(lv1, zb1, b)
        put(lv2, b, relaxed(h, beside, lanes_of(rhs, b)))
    pack_faces(lv2, xs2, zb2)
    second = exchange(1, xs2, xr2, zb2)
    start_all(second)
    pl.semaphore_wait(tok.at[0], 2)
    greet(1, 4)

    def missing(base, p, f):
        return jnp.where(pn[f, base + p] < 0, FACTOR, 0.0).astype(jnp.float32)

    def edge_weight(base, p, shape, with_z):
        lanes = lax.broadcasted_iota(jnp.int32, shape, 1)
        rows = lax.broadcasted_iota(jnp.int32, shape, 0)
        pair = []
        for i in range(2):
            w = jnp.ones(shape, jnp.float32)
            w = w - jnp.where(lanes % 16 == 0, missing(base, p, 0), 0.0)
            w = w - jnp.where(lanes % 16 == 15, missing(base, p, 1), 0.0)
            if i == 0:
                w = w - jnp.where(lanes < 16, missing(base, p, 2), 0.0)
            else:
                w = w - jnp.where(lanes >= 112, missing(base, p, 3), 0.0)
            if with_z is None:
                w = w - jnp.where(rows == 0, missing(base, p, 4), 0.0)
                w = w - jnp.where(rows == 15, missing(base, p, 5), 0.0)
            else:
                w = w - missing(base, p, with_z)
            pair.append(w)
        return pair

    def parent_beside(values, halo, p):
        h = both(values, p)
        g = own_ghost[p]
        low = [lane_roll(v, -15) for v in both(values, g[0])]
        high = [lane_roll(v, 15) for v in both(values, g[1])]
        xsum = x_sum(lane, h, low, high)
        ysum = y_sum(lane, h, values[1, g[2]], values[0, g[3]])
        zsum = z_sum(
            row,
            h,
            row_pair(halo, g[4]),
            row_pair(halo, g[5] + 17),
        )
        return h, [xsum[i] + ysum[i] + zsum[i] for i in range(2)]

    for p in range(PARENTS_HERE):
        put(pv1, p, edge_weight(mine, p, (16, 128), None))
        for side in range(2):
            pair = edge_weight(halo_base[side], p, (1, 128), 5 - side)
            hv[side * 17 + p, :, 0:128] = pair[0]
            hv[side * 17 + p, :, 128:256] = pair[1]
    for p in range(PARENTS_HERE):
        h, beside = parent_beside(pv1, hv, p)
        put(geo, p, relaxed(h, beside, [0.0, 0.0]))

    wait_arrivals(second)
    unpack_x(xr2)
    for b in range(LEAVES_HERE):
        h, beside = leaf_beside(lv2, zb2, b)
        put(res, b, rest(h, beside, lanes_of(rhs, b)))
    pieces = []
    for b in range(LEAVES_HERE):
        pieces.append(
            jnp.concatenate(
                [
                    res[i, b, pl.ds(0, 8, stride=2), :] + res[i, b, pl.ds(1, 8, stride=2), :]
                    for i in range(2)
                ],
                axis=1,
            )
        )
    stacked = jnp.concatenate(
        [jnp.concatenate(pieces[0:4], axis=0), jnp.concatenate(pieces[4:8], axis=0)], axis=1
    )
    oct_rows[s] = split_dot(0.5 * stacked, restrict).reshape(4, 8, 128)

    def octants(k):
        return pltpu.make_async_remote_copy(
            src_ref=oct_rows.at[s],
            dst_ref=oct_rows.at[s],
            send_sem=c_send.at[k],
            recv_sem=c_recv.at[k],
            device_id=(r, (s + k) % subs),
            device_id_type=MESH,
        )

    order = (8, 2, 10, 6, 14, 7, 9, 5, 11, 3, 13, 4, 12, 1, 15)
    for k in order:
        octants(k).start()

    pl.semaphore_wait(tok.at[1], 2)
    greet(2, 8)

    leaf_parent = []
    leaf_octant = []
    flat = numbers((8, 512), 1) * 8 + numbers((8, 512), 0)
    leaf_ids = chv[...]
    for b in range(LEAVES_HERE):
        found = jnp.sum(jnp.where(leaf_ids == here * 8 + b, flat, 0)) - mine * 8
        found = jnp.clip(found, 0, 127)
        leaf_parent.append(found >> 3)
        leaf_octant.append(found & 7)
    slot_parent = [jnp.int32(0)] * 3
    slot_filled = [jnp.int32(0)] * 3
    seen = jnp.int32(0)
    for p in range(PARENTS_HERE):
        owned = ow[mine + p] == s
        for k in range(3):
            take = jnp.logical_and(owned, seen == k)
            slot_parent[k] = jnp.where(take, p, slot_parent[k])
            slot_filled[k] = jnp.where(take, 1, slot_filled[k])
        seen = seen + jnp.where(owned, 1, 0)

    for k in order:
        octants(k).wait_recv()

    for p in range(PARENTS_HERE):
        for oz in range(2):
            for oy in range(2):
                parts = []
                for ox in range(2):
                    n = jnp.clip(ch[4 * oz + 2 * oy + ox, mine + p] - mine * 8, 0, 127)
                    tile = oct_rows[n >> 3, n & 3]
                    wanted = ((n >> 2) & 1) == ox
                    parts.append(jnp.where(wanted, tile, lane_roll(tile, 8 if ox else -8)))
                src[oy, p, oz * 8 : oz * 8 + 8, :] = jnp.where(
                    column8 < 8, parts[0], parts[1]
                )

    for layer in range(2):
        for i in range(2):
            hsend[0, layer, :, i * 128 : i * 128 + 128] = src[i, :, layer, :]
            hsend[1, layer, :, i * 128 : i * 128 + 128] = src[i, :, 15 - layer, :]

    def halo_copy(direction):
        step = -1 if direction == 0 else 1
        return pltpu.make_async_remote_copy(
            src_ref=hsend.at[direction],
            dst_ref=hrecv.at[1 - direction],
            send_sem=d_send.at[direction],
            recv_sem=d_recv.at[direction],
            device_id=((r + step + ranges) % ranges, s),
            device_id_type=MESH,
        )

    halos = (
        (r > 0, r < ranges - 1, halo_copy(0)),
        (r < ranges - 1, r > 0, halo_copy(1)),
    )
    start_all(halos)

    total = jnp.zeros((16, 128), jnp.float32)
    for p in range(PARENTS_HERE):
        g = both(geo, p)
        v = both(src, p)
        total = total + g[0] * v[0] + g[1] * v[1]
    msend[0] = jnp.sum(total, axis=0, keepdims=True)
    pair_device = (r + 1 - 2 * (r % 2), s)

    def mean_copy(k):
        return pltpu.make_async_remote_copy(
            src_ref=msend.at[0 if k == 0 else 1],
            dst_ref=mrecv.at[k],
            send_sem=m_send.at[k],
            recv_sem=m_recv.at[k],
            device_id=pair_device if k == 0 else ((r + 2 * k) % ranges, s),
            device_id_type=MESH,
        )

    mean_copy(0).start()
    for p in range(PARENTS_HERE):
        put(pv1, p, [FACTOR * v for v in both(src, p)])
    pl.semaphore_wait(tok.at[2], 2)
    mean_copy(0).wait_recv()
    msend[1] = msend[0] + mrecv[0]
    for k in range(1, 16):
        mean_copy(k).start()

    root_row = numbers((24, 128), 0)
    root_lane = numbers((24, 128), 1)
    depth = root_row + 4 * r - 8
    domain = (depth >= 0) & (depth < 4 * ranges) & (root_row < 20)

    def root_sweeps(source):
        w = [FACTOR * v for v in source]
        for _ in range(SWEEPS - 1):
            up = [lane_roll(v, 32) for v in w]
            down = [lane_roll(v, -32) for v in w]
            ysum = [
                jnp.where(root_lane < 32, 0.0, up[0])
                + jnp.where(root_lane >= 96, down[1], down[0]),
                jnp.where(root_lane < 32, up[0], up[1])
                + jnp.where(root_lane >= 96, 0.0, down[1]),
            ]
            fresh = []
            for i in range(2):
                xsum = jnp.where(root_lane % 32 == 0, 0.0, lane_roll(w[i], 1)) + jnp.where(
                    root_lane % 32 == 31, 0.0, lane_roll(w[i], -1)
                )
                zsum = row_roll(w[i], 1) + row_roll(w[i], -1)
                fresh.append(
                    jnp.where(
                        domain,
                        w[i]
                        + FACTOR * (source[i] - (6.0 * w[i] - (xsum + ysum[i] + zsum))),
                        0.0,
                    )
                )
            w = fresh
        return w

    ones = jnp.where(domain, 1.0, 0.0).astype(jnp.float32)
    flat_root = root_sweeps([ones, ones])

    wait_arrivals(halos)

    def gather(ref, index_of):
        for q in range(PARENTS_HERE):
            rows_tmp[q : q + 1, :] = ref[index_of(q)]
        return flat_pair(rows_tmp, slice(0, 16))

    def spread(ref, side, pair):
        put_flat(rows_tmp, slice(0, 16), pair)
        for q in range(PARENTS_HERE):
            ref[side * 17 + q] = rows_tmp[q : q + 1, :]

    for side in range(2):
        spread(hv, side, [FACTOR * hrecv[side, 0, :, i * 128 : i * 128 + 128] for i in range(2)])
    for p in range(PARENTS_HERE):
        put_row(own_rows, p, [pv1[i, p, 0:1, :] for i in range(2)])
        put_row(own_rows, 17 + p, [pv1[i, p, 15:16, :] for i in range(2)])
    for side in range(2):
        near = [hrecv[side, 0, :, i * 128 : i * 128 + 128] for i in range(2)]
        deep = [hrecv[side, 1, :, i * 128 : i * 128 + 128] for i in range(2)]
        h = [FACTOR * v for v in near]
        ghost = halo_ghost[side]
        low = [lane_roll(v, -15) for v in gather(hv, lambda q: ghost[q][0] + side * 17)]
        high = [lane_roll(v, 15) for v in gather(hv, lambda q: ghost[q][1] + side * 17)]
        xsum = x_sum(lane, h, low, high)
        below = gather(hv, lambda q: ghost[q][2] + side * 17)[1]
        above = gather(hv, lambda q: ghost[q][3] + side * 17)[0]
        ysum = y_sum(lane, h, below, above)
        touching = gather(own_rows, lambda q: halo_own[side][q] + side * 17)
        beside = [xsum[i] + ysum[i] + FACTOR * deep[i] + touching[i] for i in range(2)]
        put_flat(halo_two, slice(side * 16, side * 16 + 16), relaxed(h, beside, near))
        spread(h2, side, flat_pair(halo_two, slice(side * 16, side * 16 + 16)))

    for p in range(PARENTS_HERE):
        h, beside = parent_beside(pv1, hv, p)
        put(pv2, p, relaxed(h, beside, both(src, p)))
    for p in range(PARENTS_HERE):
        h, beside = parent_beside(pv2, h2, p)
        put(pv4, p, rest(h, beside, both(src, p)))
    for p in range(PARENTS_HERE):
        for i in range(2):
            quad = pv4[i, p, pl.ds(0, 4, stride=4), :]
            for t in range(1, 4):
                quad = quad + pv4[i, p, pl.ds(t, 4, stride=4), :]
            zq[p * 4 : p * 4 + 4, i * 128 : i * 128 + 128] = 0.25 * quad
    zq[...] = split_dot(zq[...], coarse_table)
    place_lane = [numbers((4, 128), 1) % 32 // 4 + 8 * i for i in range(2)]
    pair = [jnp.zeros((4, 128), jnp.float32) for _ in range(2)]
    for p in range(PARENTS_HERE):
        place = places[mine + p] - mine
        for i in range(2):
            pair[i] = jnp.where(
                place_lane[i] == place, zq[p * 4 : p * 4 + 4, i * 128 : i * 128 + 128], pair[i]
            )
    slab[:, 0:128] = pair[0]
    slab[:, 128:256] = pair[1]

    shifts = (1, -1, 2, -2)

    def slab_copy(k):
        return pltpu.make_async_remote_copy(
            src_ref=slab,
            dst_ref=rbuf.at[2 - shifts[k]],
            send_sem=f_send.at[k],
            recv_sem=f_recv.at[k],
            device_id=((r + shifts[k] + ranges) % ranges, s),
            device_id_type=MESH,
        )

    slabs = tuple(
        (
            (r + d < ranges) if d > 0 else (r + d >= 0),
            (r - d >= 0) if d > 0 else (r - d < ranges),
            slab_copy(k),
        )
        for k, d in enumerate(shifts)
    )
    start_all(slabs)
    wait_arrivals(slabs)
    for slot in range(5):
        rw[slot * 4 : slot * 4 + 4, :] = slab[...] if slot == 2 else rbuf[slot]
    rw[20:24, :] = jnp.zeros((4, 256), jnp.float32)
    root = root_sweeps([jnp.where(domain, v, 0.0) for v in flat_pair(rw, slice(0, 24))])
    for k in range(1, 16):
        mean_copy(k).wait_recv()
    sums = msend[1]
    for k in range(1, 16):
        sums = sums + mrecv[k]
    mean = jnp.sum(sums) * (0.25 / (1024.0 * ranges))
    put_flat(rw, slice(0, 24), [root[i] - mean * flat_root[i] for i in range(2)])

    wide_lane = [numbers((4, 128), 1) % 32 // 4 + 8 * i for i in range(2)]
    for p in range(PARENTS_HERE):
        for i in range(2):
            lanes = slice(i * 128, i * 128 + 128)
            wm[p * 4 : p * 4 + 4, lanes] = jnp.where(
                wide_lane[i] == places[mine + p] - mine, rw[8:12, lanes], 0.0
            )
            wm[64 + p : 65 + p, lanes] = jnp.where(
                wide_lane[i][0:1] == places[lower + p] - lower, rw[7:8, lanes], 0.0
            )
            wm[80 + p : 81 + p, lanes] = jnp.where(
                wide_lane[i][0:1] == places[upper + p] - upper, rw[12:13, lanes], 0.0
            )
    we[...] = split_dot(wm[...], widen_table)
    for side in range(2):
        base = 64 + 16 * side
        rows = slice(side * 16, side * 16 + 16)
        grown = flat_pair(we, slice(base, base + 16))
        spread(h2, side, [v + grown[i] for i, v in enumerate(flat_pair(halo_two, rows))])
    for p in range(PARENTS_HERE):
        pair = []
        for i in range(2):
            lanes = slice(i * 128, i * 128 + 128)
            grown = jnp.where(
                row < 8,
                jnp.where(row < 4, we[p * 4 : p * 4 + 1, lanes], we[p * 4 + 1 : p * 4 + 2, lanes]),
                jnp.where(
                    row < 12, we[p * 4 + 2 : p * 4 + 3, lanes], we[p * 4 + 3 : p * 4 + 4, lanes]
                ),
            )
            pair.append(pv2[i, p] + grown)
        put(pv3, p, pair)
    for p in range(PARENTS_HERE):
        h, beside = parent_beside(pv3, h2, p)
        put(pv4, p, relaxed(h, beside, both(src, p)))

    tiles = []
    for b in range(LEAVES_HERE):
        own = both(pv4, leaf_parent[b])
        side = jnp.where(((leaf_octant[b] >> 1) & 1) == 1, own[1], own[0])
        tiles.append(jnp.where((leaf_octant[b] >> 2) == 1, side[8:16], side[0:8]))
    lw[...] = split_dot(jnp.concatenate(tiles, axis=0), leaf_table)
    for b in range(LEAVES_HERE):
        piece = lw[b * 8 : b * 8 + 8, :]
        for t in range(2):
            rows = pl.ds(t, 8, stride=2)
            for i in range(2):
                lv3[i, b, rows, :] = lv2[i, b, rows, :] + piece[:, i * 128 : i * 128 + 128]
    pack_faces(lv3, xs3, zb3)
    third = exchange(2, xs3, xr3, zb3)
    start_all(third)
    for k in range(3):
        own = both(pv4, slot_parent[k])
        for i in range(2):
            parent_out[k, :, i * 128 : i * 128 + 128] = jnp.where(
                slot_filled[k] == 1, own[i], 0.0
            )
    wait_arrivals(third)
    unpack_x(xr3)
    for b in range(LEAVES_HERE):
        h, beside = leaf_beside(lv3, zb3, b)
        pair = relaxed(h, beside, lanes_of(rhs, b))
        for i in range(2):
            leaf_out[b, :, i * 128 : i * 128 + 128] = pair[i]

    for copies in (first, second, third, halos, slabs):
        wait_departures(copies)
    for k in range(1, 16):
        octants(k).wait_send()
    for k in range(16):
        mean_copy(k).wait_send()


def local(rhs, leaf_neighbors, parent_neighbors, children, owners, parent_places):
    f32 = jnp.float32
    vmem = pl.BlockSpec(memory_space=pltpu.VMEM)
    smem = pl.BlockSpec(memory_space=pltpu.SMEM)
    kids = children.T
    return pl.pallas_call(
        kernel,
        out_shape=(
            jax.ShapeDtypeStruct((8, 16, 256), f32),
            jax.ShapeDtypeStruct((3, 16, 256), f32),
        ),
        in_specs=[vmem, smem, smem, smem, smem, smem, vmem],
        out_specs=(vmem, vmem),
        scratch_shapes=[
            pltpu.VMEM((2, 9, 16, 128), f32),
            pltpu.VMEM((2, 9, 16, 128), f32),
            pltpu.VMEM((2, 9, 16, 128), f32),
            pltpu.VMEM((2, 8, 256), f32),
            pltpu.VMEM((2, 8, 256), f32),
            pltpu.VMEM((2, 8, 256), f32),
            pltpu.VMEM((2, 8, 256), f32),
            pltpu.VMEM((2, 8, 256), f32),
            pltpu.VMEM((2, 8, 256), f32),
            pltpu.VMEM((2, 2, 9, 16, 128), f32),
            pltpu.VMEM((33, 1, 256), f32),
            pltpu.VMEM((33, 1, 256), f32),
            pltpu.VMEM((33, 1, 256), f32),
            pltpu.VMEM((2, 8, 16, 128), f32),
            pltpu.VMEM((16, 4, 8, 128), f32),
            pltpu.VMEM((2, 16, 16, 128), f32),
            pltpu.VMEM((2, 17, 16, 128), f32),
            pltpu.VMEM((2, 17, 16, 128), f32),
            pltpu.VMEM((2, 17, 16, 128), f32),
            pltpu.VMEM((2, 16, 16, 128), f32),
            pltpu.VMEM((2, 17, 16, 128), f32),
            pltpu.VMEM((2, 2, 16, 256), f32),
            pltpu.VMEM((2, 2, 16, 256), f32),
            pltpu.VMEM((34, 1, 256), f32),
            pltpu.VMEM((34, 1, 256), f32),
            pltpu.VMEM((34, 1, 256), f32),
            pltpu.VMEM((32, 256), f32),
            pltpu.VMEM((16, 256), f32),
            pltpu.VMEM((64, 256), f32),
            pltpu.VMEM((4, 256), f32),
            pltpu.VMEM((5, 4, 256), f32),
            pltpu.VMEM((24, 256), f32),
            pltpu.VMEM((96, 256), f32),
            pltpu.VMEM((96, 256), f32),
            pltpu.VMEM((2, 1, 128), f32),
            pltpu.VMEM((16, 1, 128), f32),
            pltpu.VMEM((64, 256), f32),
            pltpu.SemaphoreType.DMA((3, 4)),
            pltpu.SemaphoreType.DMA((3, 4)),
            pltpu.SemaphoreType.DMA((16,)),
            pltpu.SemaphoreType.DMA((16,)),
            pltpu.SemaphoreType.DMA((2,)),
            pltpu.SemaphoreType.DMA((2,)),
            pltpu.SemaphoreType.DMA((4,)),
            pltpu.SemaphoreType.DMA((4,)),
            pltpu.SemaphoreType.DMA((16,)),
            pltpu.SemaphoreType.DMA((16,)),
            pltpu.SemaphoreType.REGULAR((3,)),
        ],
        compiler_params=pltpu.CompilerParams(collective_id=0, has_side_effects=True),
        name="vcycle",
    )(
        rhs,
        leaf_neighbors,
        parent_neighbors.T,
        kids,
        owners,
        parent_places,
        kids,
    )


def solution(mesh):
    in_specs = (P(("blk", "sub"), None, None), P(("blk", "sub"), None), P(), P(), P(), P())
    out_specs = (P(("blk", "sub"), None, None), P(("blk", "sub"), None, None))
    return jax.shard_map(local, mesh=mesh, in_specs=in_specs, out_specs=out_specs, check_vma=False)
```

time: 185 us -> 47.4 us (0.26); the launches traced: 182 us -> 47.2 us
  starting transfers between devices: 77.8 us -> 0 us
  local copies, waits for them, and re-layouts: 56.2 us -> 2.2 us
  Pallas kernels: 0 us -> 44.3 us
  waiting for transfers between devices: 28.1 us -> 0 us
  other arithmetic: 10.5 us -> 0 us
  matrix products: 6.12 us -> 0 us
  between operations: 3.06 us -> 0.65 us
    ppermute x18 -> x0, starting transfers between devices: 48 us -> none  [the longest x9 30 us: extended(): lax.ppermute(lax.slice_in_dim(block, block.shape[dim] - width, None, axis...]
    pallas_call x0 -> x1, Pallas kernels: none -> 44.3 us  [local(): pl.pallas_call(kernel, out_shape=(jax.ShapeDtypeStruct((8, 16, 256), f32)...]
    all_to_all x2 -> x0, starting transfers between devices: 29.8 us -> none  [copy_for_each(): lax.all_to_all(jnp.broadcast_to(array[None], (peers, *array.shape)), axis...]
    all_to_all x2 -> x0, waiting for transfers between devices: 23.4 us -> none  [copy_for_each(): lax.all_to_all(jnp.broadcast_to(array[None], (peers, *array.shape)), axis...]
    reshape x28 -> x0, local copies, waits for them, and re-layouts: 10.7 us -> none  [the longest x1 5.64 us: local(): root_values.reshape(blk_count, 4, side_y, 4, side_x, 4)]
    transpose x3 -> x0, local copies, waits for them, and re-layouts: 10 us -> none  [the longest x1 9.71 us: local(): root_back = root_values.reshape(blk_count, 4, side_y, 4, side_x, 4).trans...]
    sub x3 -> x0, local copies, waits for them, and re-layouts: 9.62 us -> none  [the longest x2 9.55 us: local(): root_source = root_source - jnp.mean(root_source)]
    slice x33 -> x0, local copies, waits for them, and re-layouts: 8.14 us -> none  [the longest x6 3.31 us: block_faces(): values[:, :, 15::16].reshape(blocks, 256)]
  transfers between devices with their start and end apart: 20 -> 0, of which waited for: 4 -> 0; matrix products, arithmetic and copies ran while one was open for 8% -> 0% of each run, Pallas kernels for 0% -> 0%
where the time goes in v1:
time: 47.4 us; the launch traced here: 47.2 us
  Pallas kernels  44.3 us (93%)
  local copies, waits for them, and re-layouts  2.2 us (5%)
  between operations  0.65 us (1%)
    pallas_call x1, Pallas kernels, local(): pl.pallas_call(kernel, out_shape=(jax.ShapeDtypeStruct((8, 16, 256), f32)...  44.3 us
    unnamed x4, local copies, waits for them, and re-layouts  2.2 us

profile of v1, /device:TPU:1, one launch (start us, length us, event | category | flops | bytes accessed | tf_op | source)
XLA Modules:
  0.0 47.2 jit_solution(15814670768407474003)
XLA Ops:
  0.6 44.3 %vcycle.1 = (f32[8,16,256]{2,1,0:T(8,128)}, f32[3,16,256]{2,1,0:T(8,128)}) custom-call(f32[8,16,256]{2,1,0:T(8,128)} %rhs.1, s32[8,6]{1,0:T(8,128)} %ln.1, s32[6,512]{1,0:T(8,128)} %bitcast.4, s32[8,512]{1,0:T(8,128)} %bitcast.2, s32[512]{0:T(512)} %ow.1, s32[512]{0:T(512)} %places.1, s32[8,512]{1,0:T(8,128)} %bitcast.3), custom_call_target="tpu_custom_call" | custom-call | tf_op jit(solution)/shard_map/vcycle/pallas_call | solution.py:760
  44.9 0.0 copy-start
  45.0 1.6 %copy.10 = f32[8,16,256]{2,1,0:T(8,128)} copy(f32[8,16,256]{2,1,0:T(8,128)} %get-tuple-element.4) | data formatting | bytes 262144
  46.5 0.0 copy-done
  46.5 0.6 %copy.11 = f32[3,16,256]{2,1,0:T(8,128)} copy(f32[3,16,256]{2,1,0:T(8,128)S(1)} %copy-done) | data formatting | bytes 98304
Async XLA Ops:
  44.9 1.6 %copy-start = (f32[3,16,256]{2,1,0:T(8,128)S(1)}, f32[3,16,256]{2,1,0:T(8,128)}, u32[]{:S(2)}) copy-start(f32[3,16,256]{2,1,0:T(8,128)} %get-tuple-element.5) | copy-start | bytes 147460

commit v2 on v1

--- a/solution.py
+++ b/solution.py
@@ -89,6 +89,14 @@
 
 
 def kernel(
+    rhs_in,
+    ln_in,
+    pn_in,
+    ch_in,
+    ow_in,
+    places_in,
+    leaf_out,
+    parent_out,
     rhs,
     ln,
     pn,
@@ -96,8 +104,15 @@
     ow,
     places,
     chv,
-    leaf_out,
-    parent_out,
+    load_sem,
+    ghost_table,
+    pe3,
+    pe4,
+    le3,
+    le4,
+    xs4,
+    xr4,
+    zb4,
     lv1,
     lv2,
     lv3,
@@ -134,6 +149,7 @@
     we,
     msend,
     mrecv,
+    precv,
     lw,
     a_send,
     a_recv,
@@ -145,19 +161,74 @@
     f_recv,
     m_send,
     m_recv,
+    p_send,
+    p_recv,
     tok,
 ):
     ranges = lax.axis_size("blk")
     subs = lax.axis_size("sub")
     r = lax.axis_index("blk")
     s = lax.axis_index("sub")
+    pairs = (
+        (rhs_in, rhs),
+        (ln_in, ln),
+        (pn_in, pn),
+        (ch_in, ch),
+        (ch_in, chv),
+        (ow_in, ow),
+        (places_in, places),
+    )
+    loads = [
+        pltpu.make_async_copy(source, target, load_sem.at[k])
+        for k, (source, target) in enumerate(pairs)
+    ]
+    for load in loads:
+        load.start()
+
     barrier = pltpu.get_barrier_semaphore()
-    for k in range(1, 16):
-        pl.semaphore_signal(barrier, inc=1, device_id=(r, (s + k) % subs), device_id_type=MESH)
-    for d in (1, -1, 2, -2):
-        pl.semaphore_signal(
-            barrier, inc=1, device_id=((r + d + ranges) % ranges, s), device_id_type=MESH
-        )
+
+    def exists(d):
+        return (r + d < ranges) if d > 0 else (r + d >= 0)
+
+    def signal_range(semaphore, distances):
+        for d in distances:
+
+            @pl.when(exists(d))
+            def _():
+                pl.semaphore_signal(
+                    semaphore,
+                    inc=1,
+                    device_id=((r + d + ranges) % ranges, s),
+                    device_id_type=MESH,
+                )
+
+    def signal_sub(semaphore, distances):
+        for d in distances:
+            pl.semaphore_signal(
+                semaphore,
+                inc=1,
+                device_id=(r, (s + d + subs) % subs),
+                device_id_type=MESH,
+            )
+
+    signal_range(barrier, (1, -1, 2, -2))
+    signal_sub(barrier, (1, -1, 4, -4))
+    middle = ranges // 2
+    for k in range(2, 16):
+
+        @pl.when((r < middle) & (r + 2 * k < ranges))
+        def _():
+            pl.semaphore_signal(
+                barrier,
+                inc=1,
+                device_id=((r + 2 * k) % ranges, s),
+                device_id_type=MESH,
+            )
+
+    greetings = 4 + sum(exists(d).astype(jnp.int32) for d in (1, -1, 2, -2))
+    greetings = greetings + sum(
+        ((r - 2 * k >= 0) & (r - 2 * k < middle)).astype(jnp.int32) for k in range(2, 16)
+    )
 
     lane = lax.broadcasted_iota(jnp.int32, (16, 128), 1)
     row = lax.broadcasted_iota(jnp.int32, (16, 128), 0)
@@ -166,6 +237,160 @@
     zero_half = jnp.zeros((16, 128), jnp.float32)
     zeros = [zero_half, zero_half]
 
+    def pack_faces(values, xs, zb):
+        for h in range(2):
+            low = jnp.zeros((8, 128), jnp.float32)
+            high = jnp.zeros((8, 128), jnp.float32)
+            for b in range(LEAVES_HERE):
+                for part in range(2):
+                    v = values[h, b, part * 8 : part * 8 + 8, :]
+                    k = part * 8 + b
+                    low = jnp.where(column8 == k, lane_roll(v, k), low)
+                    high = jnp.where(column8 == k, lane_roll(v, k - 15), high)
+            xs[0, :, h * 128 : h * 128 + 128] = low
+            xs[1, :, h * 128 : h * 128 + 128] = high
+        for b in range(LEAVES_HERE):
+            put_row(zb, b, [values[i, b, 0:1, :] for i in range(2)])
+            put_row(zb, 8 + b, [values[i, b, 15:16, :] for i in range(2)])
+        zb[32] = jnp.zeros((1, 256), jnp.float32)
+
+    def exchange(step, xs, xr, zb):
+        def remote(source, target, slot, device):
+            return pltpu.make_async_remote_copy(
+                src_ref=source,
+                dst_ref=target,
+                send_sem=a_send.at[step, slot],
+                recv_sem=a_recv.at[step, slot],
+                device_id=device,
+                device_id_type=MESH,
+            )
+
+        return (
+            (s > 0, s < subs - 1, remote(xs.at[0], xr.at[1], 0, (r, (s + subs - 1) % subs))),
+            (s < subs - 1, s > 0, remote(xs.at[1], xr.at[0], 1, (r, (s + 1) % subs))),
+            (
+                r > 0,
+                r < ranges - 1,
+                remote(zb.at[0:8], zb.at[24:32], 2, ((r + ranges - 1) % ranges, s)),
+            ),
+            (
+                r < ranges - 1,
+                r > 0,
+                remote(zb.at[8:16], zb.at[16:24], 3, ((r + 1) % ranges, s)),
+            ),
+        )
+
+    def start_all(copies):
+        for sends, _, copy in copies:
+
+            @pl.when(sends)
+            def _():
+                copy.start()
+
+    def wait_arrivals(copies):
+        for _, arrives, copy in copies:
+
+            @pl.when(arrives)
+            def _():
+                copy.wait_recv()
+
+    def wait_departures(copies):
+        for sends, _, copy in copies:
+
+            @pl.when(sends)
+            def _():
+                copy.wait_send()
+
+    def unpack_x(xr):
+        for h in range(2):
+            lanes = slice(h * 128, h * 128 + 128)
+            below = xr[0, :, lanes]
+            above = xr[1, :, lanes]
+            for j in range(LEAVES_HERE):
+                for part in range(2):
+                    k = part * 8 + j
+                    rows = slice(part * 8, part * 8 + 8)
+                    xt[0, h, j, rows, :] = lane_roll(below, -k)
+                    xt[1, h, j, rows, :] = lane_roll(above, 15 - k)
+
+    def leaf_beside(values, zb, b):
+        h = both(values, b)
+        low = [xt[0, i, leaf_x[b][0]] for i in range(2)]
+        high = [xt[1, i, leaf_x[b][1]] for i in range(2)]
+        xsum = x_sum(lane, h, low, high)
+        ysum = y_sum(
+            lane,
+            h,
+            values[1, leaf_y[b][0]],
+            values[0, leaf_y[b][1]],
+        )
+        zsum = z_sum(
+            row,
+            h,
+            row_pair(zb, leaf_z[b][0]),
+            row_pair(zb, leaf_z[b][1]),
+        )
+        return h, [xsum[i] + ysum[i] + zsum[i] for i in range(2)]
+
+    def relaxed(h, beside, forcing):
+        return [h[i] + FACTOR * (forcing[i] - (6.0 * h[i] - beside[i])) for i in range(2)]
+
+    def rest(h, beside, forcing):
+        return [forcing[i] - (6.0 * h[i] - beside[i]) for i in range(2)]
+
+    for ref in (lv1, lv2, lv3, le3):
+        put(ref, 8, zeros)
+    for ref in (pv1, pv2, pv3, pe3):
+        put(ref, 16, zeros)
+    for side in range(2):
+        xt[side, 0, 8] = zero_half
+        xt[side, 1, 8] = zero_half
+    for side in range(2):
+        for ref in (hv, h2, own_rows):
+            ref[side * 17 + 16] = jnp.zeros((1, 256), jnp.float32)
+
+    loads[0].wait()
+    for b in range(LEAVES_HERE):
+        put(lv1, b, [FACTOR * v for v in lanes_of(rhs, b)])
+    pack_faces(lv1, xs1, zb1)
+    pl.semaphore_wait(barrier, greetings)
+    first = exchange(0, xs1, xr1, zb1)
+    start_all(first)
+
+    def tell(stage):
+        distance = 2 << stage
+
+        @pl.when((r >= middle) & (r + distance < ranges))
+        def _():
+            pl.semaphore_signal(
+                tok.at[stage],
+                inc=1,
+                device_id=((r + distance) % ranges, s),
+                device_id_type=MESH,
+            )
+
+        @pl.when(r - distance >= middle)
+        def _():
+            pl.semaphore_signal(
+                tok.at[stage],
+                inc=1,
+                device_id=((r - distance + ranges) % ranges, s),
+                device_id_type=MESH,
+            )
+
+    def hear(stage):
+        distance = 2 << stage
+        peers = ((r >= middle) & (r + distance < ranges)).astype(jnp.int32)
+        peers = peers + (r - distance >= middle).astype(jnp.int32)
+
+        @pl.when(peers > 0)
+        def _():
+            pl.semaphore_wait(tok.at[stage], peers)
+
+    tell(0)
+    signal_sub(tok.at[4], (1, -1, 4, -4))
+
+    loads[1].wait()
     here = r * subs + s
     leaf_y = [[None, None] for _ in range(LEAVES_HERE)]
     leaf_x = [[None, None] for _ in range(LEAVES_HERE)]
@@ -185,136 +410,6 @@
                     n >= 0, (n & 7) + jnp.where(remote, far_base, own_base), 32
                 )
 
-    def pack_faces(values, xs, zb):
-        for h in range(2):
-            low = jnp.zeros((8, 128), jnp.float32)
-            high = jnp.zeros((8, 128), jnp.float32)
-            for b in range(LEAVES_HERE):
-                for part in range(2):
-                    v = values[h, b, part * 8 : part * 8 + 8, :]
-                    k = part * 8 + b
-                    low = jnp.where(column8 == k, lane_roll(v, k), low)
-                    high = jnp.where(column8 == k, lane_roll(v, k - 15), high)
-            xs[0, :, h * 128 : h * 128 + 128] = low
-            xs[1, :, h * 128 : h * 128 + 128] = high
-        for b in range(LEAVES_HERE):
-            put_row(zb, b, [values[i, b, 0:1, :] for i in range(2)])
-            put_row(zb, 8 + b, [values[i, b, 15:16, :] for i in range(2)])
-        zb[32] = jnp.zeros((1, 256), jnp.float32)
-
-    def exchange(step, xs, xr, zb):
-        def remote(source, target, slot, device):
-            return pltpu.make_async_remote_copy(
-                src_ref=source,
-                dst_ref=target,
-                send_sem=a_send.at[step, slot],
-                recv_sem=a_recv.at[step, slot],
-                device_id=device,
-                device_id_type=MESH,
-            )
-
-        return (
-            (s > 0, s < subs - 1, remote(xs.at[0], xr.at[1], 0, (r, (s + subs - 1) % subs))),
-            (s < subs - 1, s > 0, remote(xs.at[1], xr.at[0], 1, (r, (s + 1) % subs))),
-            (
-                r > 0,
-                r < ranges - 1,
-                remote(zb.at[0:8], zb.at[24:32], 2, ((r + ranges - 1) % ranges, s)),
-            ),
-            (
-                r < ranges - 1,
-                r > 0,
-                remote(zb.at[8:16], zb.at[16:24], 3, ((r + 1) % ranges, s)),
-            ),
-        )
-
-    def start_all(copies):
-        for sends, _, copy in copies:
-
-            @pl.when(sends)
-            def _():
-                copy.start()
-
-    def wait_arrivals(copies):
-        for _, arrives, copy in copies:
-
-            @pl.when(arrives)
-            def _():
-                copy.wait_recv()
-
-    def wait_departures(copies):
-        for sends, _, copy in copies:
-
-            @pl.when(sends)
-            def _():
-                copy.wait_send()
-
-    def unpack_x(xr):
-        for h in range(2):
-            lanes = slice(h * 128, h * 128 + 128)
-            below = xr[0, :, lanes]
-            above = xr[1, :, lanes]
-            for j in range(LEAVES_HERE):
-                for part in range(2):
-                    k = part * 8 + j
-                    rows = slice(part * 8, part * 8 + 8)
-                    xt[0, h, j, rows, :] = lane_roll(below, -k)
-                    xt[1, h, j, rows, :] = lane_roll(above, 15 - k)
-
-    def leaf_beside(values, zb, b):
-        h = both(values, b)
-        low = [xt[0, i, leaf_x[b][0]] for i in range(2)]
-        high = [xt[1, i, leaf_x[b][1]] for i in range(2)]
-        xsum = x_sum(lane, h, low, high)
-        ysum = y_sum(
-            lane,
-            h,
-            values[1, leaf_y[b][0]],
-            values[0, leaf_y[b][1]],
-        )
-        zsum = z_sum(
-            row,
-            h,
-            row_pair(zb, leaf_z[b][0]),
-            row_pair(zb, leaf_z[b][1]),
-        )
-        return h, [xsum[i] + ysum[i] + zsum[i] for i in range(2)]
-
-    def relaxed(h, beside, forcing):
-        return [h[i] + FACTOR * (forcing[i] - (6.0 * h[i] - beside[i])) for i in range(2)]
-
-    def rest(h, beside, forcing):
-        return [forcing[i] - (6.0 * h[i] - beside[i]) for i in range(2)]
-
-    for ref in (lv1, lv2, lv3):
-        put(ref, 8, zeros)
-    for ref in (pv1, pv2, pv3):
-        put(ref, 16, zeros)
-    for side in range(2):
-        xt[side, 0, 8] = zero_half
-        xt[side, 1, 8] = zero_half
-    for side in range(2):
-        for ref in (hv, h2, own_rows):
-            ref[side * 17 + 16] = jnp.zeros((1, 256), jnp.float32)
-
-    for b in range(LEAVES_HERE):
-        put(lv1, b, [FACTOR * v for v in lanes_of(rhs, b)])
-    pack_faces(lv1, xs1, zb1)
-    pl.semaphore_wait(barrier, 19)
-    first = exchange(0, xs1, xr1, zb1)
-    start_all(first)
-
-    def greet(step, distance):
-        for d in (distance, -distance):
-            pl.semaphore_signal(
-                tok.at[step],
-                inc=1,
-                device_id=((r + d + ranges) % ranges, s),
-                device_id_type=MESH,
-            )
-
-    greet(0, 2)
-
     def numbers(shape, dim):
         return lax.broadcasted_iota(jnp.int32, shape, dim)
 
@@ -344,6 +439,8 @@
         & (octant_in % 16 == (leaf_cell % 16) // 2 + (s % 2) * 8)
     )
 
+    for load in loads[2:]:
+        load.wait()
     def inside(n, base):
         return jnp.where(n >= 0, jnp.clip(n - base, 0, 15), 16)
 
@@ -357,6 +454,9 @@
         ]
         for p in range(PARENTS_HERE)
     ]
+    for p in range(PARENTS_HERE):
+        for f in range(6):
+            ghost_table[p * 6 + f] = own_ghost[p][f]
     halo_base = (lower, upper)
     halo_ghost = [
         [[inside(pn[f, base + q], base) for f in range(4)] for q in range(PARENTS_HERE)]
@@ -370,7 +470,13 @@
         for side in range(2)
     ]
 
+    hear(0)
+    tell(1)
     wait_arrivals(first)
+    hear(1)
+    tell(2)
+    pl.semaphore_wait(tok.at[4], 4)
+    signal_sub(tok.at[5], (2, -2))
     unpack_x(xr1)
     for b in range(LEAVES_HERE):
         h, beside = leaf_beside(lv1, zb1, b)
@@ -378,8 +484,6 @@
     pack_faces(lv2, xs2, zb2)
     second = exchange(1, xs2, xr2, zb2)
     start_all(second)
-    pl.semaphore_wait(tok.at[0], 2)
-    greet(1, 4)
 
     def missing(base, p, f):
         return jnp.where(pn[f, base + p] < 0, FACTOR, 0.0).astype(jnp.float32)
@@ -406,7 +510,7 @@
 
     def parent_beside(values, halo, p):
         h = both(values, p)
-        g = own_ghost[p]
+        g = own_ghost[p] if isinstance(p, int) else [ghost_table[p * 6 + f] for f in range(6)]
         low = [lane_roll(v, -15) for v in both(values, g[0])]
         high = [lane_roll(v, 15) for v in both(values, g[1])]
         xsum = x_sum(lane, h, low, high)
@@ -428,6 +532,41 @@
     for p in range(PARENTS_HERE):
         h, beside = parent_beside(pv1, hv, p)
         put(geo, p, relaxed(h, beside, [0.0, 0.0]))
+
+    leaf_parent = []
+    leaf_octant = []
+    flat = numbers((8, 512), 1) * 8 + numbers((8, 512), 0)
+    leaf_ids = chv[...]
+    for b in range(LEAVES_HERE):
+        found = jnp.sum(jnp.where(leaf_ids == here * 8 + b, flat, 0)) - mine * 8
+        found = jnp.clip(found, 0, 127)
+        leaf_parent.append(found >> 3)
+        leaf_octant.append(found & 7)
+
+    first_parent = leaf_parent[0]
+    last_parent = leaf_parent[0]
+    for n in leaf_parent[1:]:
+        first_parent = jnp.minimum(first_parent, n)
+        last_parent = jnp.maximum(last_parent, n)
+    leaf_slot = [jnp.where(n == last_parent, 1, 0) for n in leaf_parent]
+
+    def widen_leaves(parents, where_from, base, target):
+        tiles = []
+        for b in range(LEAVES_HERE):
+            own = both(parents, where_from[b])
+            side = jnp.where(((leaf_octant[b] >> 1) & 1) == 1, own[1], own[0])
+            tiles.append(jnp.where((leaf_octant[b] >> 2) == 1, side[8:16], side[0:8]))
+        lw[...] = split_dot(jnp.concatenate(tiles, axis=0), leaf_table)
+        for b in range(LEAVES_HERE):
+            piece = flat_pair(lw, slice(b * 8, b * 8 + 8))
+            for t in range(2):
+                rows = pl.ds(t, 8, stride=2)
+                for i in range(2):
+                    target[i, b, rows, :] = (
+                        piece[i] if base is None else base[i, b, rows, :] + piece[i]
+                    )
+
+    widen_leaves(geo, leaf_parent, None, lv3)
 
     wait_arrivals(second)
     unpack_x(xr2)
@@ -461,21 +600,41 @@
         )
 
     order = (8, 2, 10, 6, 14, 7, 9, 5, 11, 3, 13, 4, 12, 1, 15)
+    hear(2)
+    pl.semaphore_wait(tok.at[5], 2)
     for k in order:
         octants(k).start()
 
-    pl.semaphore_wait(tok.at[1], 2)
-    greet(2, 8)
-
-    leaf_parent = []
-    leaf_octant = []
-    flat = numbers((8, 512), 1) * 8 + numbers((8, 512), 0)
-    leaf_ids = chv[...]
+    pair_device = (r + 1 - 2 * (r % 2), s)
+
+    def mean_copy(k, distance=0):
+        return pltpu.make_async_remote_copy(
+            src_ref=msend.at[2 if k == 0 else 0],
+            dst_ref=mrecv.at[k],
+            send_sem=m_send.at[k],
+            recv_sem=m_recv.at[k],
+            device_id=pair_device if k == 0 else ((r + distance + ranges) % ranges, s),
+            device_id_type=MESH,
+        )
+
+    lower_sums = tuple(
+        (r >= 2 * k, r + 2 * k < ranges, mean_copy(k, -2 * k)) for k in range(1, 16)
+    )
+    upper_sums = tuple(
+        (r + 2 * k < ranges, r >= 2 * k, mean_copy(15 + k, 2 * k)) for k in range(1, 16)
+    )
+    total = jnp.zeros((16, 128), jnp.float32)
     for b in range(LEAVES_HERE):
-        found = jnp.sum(jnp.where(leaf_ids == here * 8 + b, flat, 0)) - mine * 8
-        found = jnp.clip(found, 0, 127)
-        leaf_parent.append(found >> 3)
-        leaf_octant.append(found & 7)
+        q = both(lv3, b)
+        v = both(res, b)
+        total = total + q[0] * v[0] + q[1] * v[1]
+    msend[0] = 0.5 * jnp.sum(total, axis=0, keepdims=True)
+    start_all(lower_sums)
+
+    @pl.when(r >= middle)
+    def _():
+        start_all(upper_sums)
+
     slot_parent = [jnp.int32(0)] * 3
     slot_filled = [jnp.int32(0)] * 3
     seen = jnp.int32(0)
@@ -487,70 +646,13 @@
             slot_filled[k] = jnp.where(take, 1, slot_filled[k])
         seen = seen + jnp.where(owned, 1, 0)
 
-    for k in order:
-        octants(k).wait_recv()
-
-    for p in range(PARENTS_HERE):
-        for oz in range(2):
-            for oy in range(2):
-                parts = []
-                for ox in range(2):
-                    n = jnp.clip(ch[4 * oz + 2 * oy + ox, mine + p] - mine * 8, 0, 127)
-                    tile = oct_rows[n >> 3, n & 3]
-                    wanted = ((n >> 2) & 1) == ox
-                    parts.append(jnp.where(wanted, tile, lane_roll(tile, 8 if ox else -8)))
-                src[oy, p, oz * 8 : oz * 8 + 8, :] = jnp.where(
-                    column8 < 8, parts[0], parts[1]
-                )
-
-    for layer in range(2):
-        for i in range(2):
-            hsend[0, layer, :, i * 128 : i * 128 + 128] = src[i, :, layer, :]
-            hsend[1, layer, :, i * 128 : i * 128 + 128] = src[i, :, 15 - layer, :]
-
-    def halo_copy(direction):
-        step = -1 if direction == 0 else 1
-        return pltpu.make_async_remote_copy(
-            src_ref=hsend.at[direction],
-            dst_ref=hrecv.at[1 - direction],
-            send_sem=d_send.at[direction],
-            recv_sem=d_recv.at[direction],
-            device_id=((r + step + ranges) % ranges, s),
-            device_id_type=MESH,
-        )
-
-    halos = (
-        (r > 0, r < ranges - 1, halo_copy(0)),
-        (r < ranges - 1, r > 0, halo_copy(1)),
-    )
-    start_all(halos)
-
-    total = jnp.zeros((16, 128), jnp.float32)
-    for p in range(PARENTS_HERE):
-        g = both(geo, p)
-        v = both(src, p)
-        total = total + g[0] * v[0] + g[1] * v[1]
-    msend[0] = jnp.sum(total, axis=0, keepdims=True)
-    pair_device = (r + 1 - 2 * (r % 2), s)
-
-    def mean_copy(k):
-        return pltpu.make_async_remote_copy(
-            src_ref=msend.at[0 if k == 0 else 1],
-            dst_ref=mrecv.at[k],
-            send_sem=m_send.at[k],
-            recv_sem=m_recv.at[k],
-            device_id=pair_device if k == 0 else ((r + 2 * k) % ranges, s),
-            device_id_type=MESH,
-        )
-
-    mean_copy(0).start()
-    for p in range(PARENTS_HERE):
-        put(pv1, p, [FACTOR * v for v in both(src, p)])
-    pl.semaphore_wait(tok.at[2], 2)
-    mean_copy(0).wait_recv()
-    msend[1] = msend[0] + mrecv[0]
-    for k in range(1, 16):
-        mean_copy(k).start()
+    kids = [
+        [jnp.clip(ch[o, mine + p] - mine * 8, 0, 127) for o in range(8)]
+        for p in range(PARENTS_HERE)
+    ]
+    kid_dev = [[n >> 3 for n in line] for line in kids]
+    kid_tile = [[n & 3 for n in line] for line in kids]
+    kid_half = [[(n >> 2) & 1 for n in line] for line in kids]
 
     root_row = numbers((24, 128), 0)
     root_lane = numbers((24, 128), 1)
@@ -588,17 +690,146 @@
     ones = jnp.where(domain, 1.0, 0.0).astype(jnp.float32)
     flat_root = root_sweeps([ones, ones])
 
+    wide_lane = [numbers((4, 128), 1) % 32 // 4 + 8 * i for i in range(2)]
+    place_own = [places[mine + p] - mine for p in range(PARENTS_HERE)]
+    place_halo = [[places[base + p] - base for p in range(PARENTS_HERE)] for base in halo_base]
+
+    def widen_root(pair):
+        put_flat(rw, slice(0, 24), pair)
+        for p in range(PARENTS_HERE):
+            for i in range(2):
+                lanes = slice(i * 128, i * 128 + 128)
+                wm[p * 4 : p * 4 + 4, lanes] = jnp.where(
+                    wide_lane[i] == place_own[p], rw[8:12, lanes], 0.0
+                )
+                wm[64 + p : 65 + p, lanes] = jnp.where(
+                    wide_lane[i][0:1] == place_halo[0][p], rw[7:8, lanes], 0.0
+                )
+                wm[80 + p : 81 + p, lanes] = jnp.where(
+                    wide_lane[i][0:1] == place_halo[1][p], rw[12:13, lanes], 0.0
+                )
+        we[...] = split_dot(wm[...], widen_table)
+
+    def widened(p):
+        pair = []
+        for i in range(2):
+            lanes = slice(i * 128, i * 128 + 128)
+            lines = [we[p * 4 + k : p * 4 + k + 1, lanes] for k in range(4)]
+            pair.append(
+                jnp.where(
+                    row < 8,
+                    jnp.where(row < 4, lines[0], lines[1]),
+                    jnp.where(row < 12, lines[2], lines[3]),
+                )
+            )
+        return pair
+
+    def spread(ref, side, pair):
+        put_flat(rows_tmp, slice(0, 16), pair)
+        for q in range(PARENTS_HERE):
+            ref[side * 17 + q] = rows_tmp[q : q + 1, :]
+
+    def column_copy(k):
+        return pltpu.make_async_remote_copy(
+            src_ref=msend.at[1],
+            dst_ref=precv.at[k],
+            send_sem=p_send.at[k],
+            recv_sem=p_recv.at[k],
+            device_id=(r, (s + k) % subs),
+            device_id_type=MESH,
+        )
+
+
+    def column_sums(now):
+        @pl.when(now)
+        def _():
+            wait_arrivals(lower_sums)
+
+            @pl.when(r < middle)
+            def _():
+                start_all(upper_sums)
+
+            wait_arrivals(upper_sums)
+            sums = msend[0]
+            for k in range(1, 16):
+                sums = sums + jnp.where(r + 2 * k < ranges, mrecv[k], 0.0)
+                sums = sums + jnp.where(r >= 2 * k, mrecv[15 + k], 0.0)
+            msend[1] = sums
+            for k in order:
+                column_copy(k).start()
+
+    def plane_sums(now):
+        @pl.when(now)
+        def _():
+            for k in order:
+                column_copy(k).wait_recv()
+            sums = msend[1]
+            for k in range(1, 16):
+                sums = sums + precv[k]
+            msend[2] = sums
+            mean_copy(0).start()
+
+
+    widen_root(flat_root)
+    for side in range(2):
+        spread(h2, side, flat_pair(we, slice(64 + 16 * side, 80 + 16 * side)))
+    for p in range(PARENTS_HERE):
+        put(pe3, p, widened(p))
+    for p in range(PARENTS_HERE):
+        h, beside = parent_beside(pe3, h2, p)
+        put(pe4, p, relaxed(h, beside, [0.0, 0.0]))
+    widen_leaves(pe4, leaf_parent, None, le3)
+    pack_faces(le3, xs4, zb4)
+    fourth = exchange(3, xs4, xr4, zb4)
+    start_all(fourth)
+
+    for k in order:
+        octants(k).wait_recv()
+
+    for p in range(PARENTS_HERE):
+        for oz in range(2):
+            for oy in range(2):
+                parts = []
+                for ox in range(2):
+                    o = 4 * oz + 2 * oy + ox
+                    tile = oct_rows[kid_dev[p][o], kid_tile[p][o]]
+                    wanted = kid_half[p][o] == ox
+                    parts.append(jnp.where(wanted, tile, lane_roll(tile, 8 if ox else -8)))
+                src[oy, p, oz * 8 : oz * 8 + 8, :] = jnp.where(
+                    column8 < 8, parts[0], parts[1]
+                )
+
+    for layer in range(2):
+        for i in range(2):
+            hsend[0, layer, :, i * 128 : i * 128 + 128] = src[i, :, layer, :]
+            hsend[1, layer, :, i * 128 : i * 128 + 128] = src[i, :, 15 - layer, :]
+
+    def halo_copy(direction):
+        step = -1 if direction == 0 else 1
+        return pltpu.make_async_remote_copy(
+            src_ref=hsend.at[direction],
+            dst_ref=hrecv.at[1 - direction],
+            send_sem=d_send.at[direction],
+            recv_sem=d_recv.at[direction],
+            device_id=((r + step + ranges) % ranges, s),
+            device_id_type=MESH,
+        )
+
+    halos = (
+        (r > 0, r < ranges - 1, halo_copy(0)),
+        (r < ranges - 1, r > 0, halo_copy(1)),
+    )
+    start_all(halos)
+
+    for p in range(PARENTS_HERE):
+        put(pv1, p, [FACTOR * v for v in both(src, p)])
+
     wait_arrivals(halos)
 
     def gather(ref, index_of):
         for q in range(PARENTS_HERE):
             rows_tmp[q : q + 1, :] = ref[index_of(q)]
         return flat_pair(rows_tmp, slice(0, 16))
-
-    def spread(ref, side, pair):
-        put_flat(rows_tmp, slice(0, 16), pair)
-        for q in range(PARENTS_HERE):
-            ref[side * 17 + q] = rows_tmp[q : q + 1, :]
 
     for side in range(2):
         spread(hv, side, [FACTOR * hrecv[side, 0, :, i * 128 : i * 128 + 128] for i in range(2)])
@@ -666,106 +897,103 @@
         for k, d in enumerate(shifts)
     )
     start_all(slabs)
+    wait_arrivals(fourth)
+    unpack_x(xr4)
+    for b in range(LEAVES_HERE):
+        h, beside = leaf_beside(le3, zb4, b)
+        put(le4, b, relaxed(h, beside, [0.0, 0.0]))
+
+    column_sums(r < middle)
     wait_arrivals(slabs)
     for slot in range(5):
         rw[slot * 4 : slot * 4 + 4, :] = slab[...] if slot == 2 else rbuf[slot]
     rw[20:24, :] = jnp.zeros((4, 256), jnp.float32)
     root = root_sweeps([jnp.where(domain, v, 0.0) for v in flat_pair(rw, slice(0, 24))])
-    for k in range(1, 16):
-        mean_copy(k).wait_recv()
-    sums = msend[1]
-    for k in range(1, 16):
-        sums = sums + mrecv[k]
-    mean = jnp.sum(sums) * (0.25 / (1024.0 * ranges))
-    put_flat(rw, slice(0, 24), [root[i] - mean * flat_root[i] for i in range(2)])
-
-    wide_lane = [numbers((4, 128), 1) % 32 // 4 + 8 * i for i in range(2)]
-    for p in range(PARENTS_HERE):
-        for i in range(2):
-            lanes = slice(i * 128, i * 128 + 128)
-            wm[p * 4 : p * 4 + 4, lanes] = jnp.where(
-                wide_lane[i] == places[mine + p] - mine, rw[8:12, lanes], 0.0
-            )
-            wm[64 + p : 65 + p, lanes] = jnp.where(
-                wide_lane[i][0:1] == places[lower + p] - lower, rw[7:8, lanes], 0.0
-            )
-            wm[80 + p : 81 + p, lanes] = jnp.where(
-                wide_lane[i][0:1] == places[upper + p] - upper, rw[12:13, lanes], 0.0
-            )
-    we[...] = split_dot(wm[...], widen_table)
+    widen_root(root)
     for side in range(2):
         base = 64 + 16 * side
         rows = slice(side * 16, side * 16 + 16)
         grown = flat_pair(we, slice(base, base + 16))
         spread(h2, side, [v + grown[i] for i, v in enumerate(flat_pair(halo_two, rows))])
     for p in range(PARENTS_HERE):
-        pair = []
-        for i in range(2):
-            lanes = slice(i * 128, i * 128 + 128)
-            grown = jnp.where(
-                row < 8,
-                jnp.where(row < 4, we[p * 4 : p * 4 + 1, lanes], we[p * 4 + 1 : p * 4 + 2, lanes]),
-                jnp.where(
-                    row < 12, we[p * 4 + 2 : p * 4 + 3, lanes], we[p * 4 + 3 : p * 4 + 4, lanes]
-                ),
-            )
-            pair.append(pv2[i, p] + grown)
-        put(pv3, p, pair)
-    for p in range(PARENTS_HERE):
+        grown = widened(p)
+        put(pv3, p, [pv2[i, p] + grown[i] for i in range(2)])
+
+    def parent_final(slot, p):
         h, beside = parent_beside(pv3, h2, p)
-        put(pv4, p, relaxed(h, beside, both(src, p)))
-
-    tiles = []
-    for b in range(LEAVES_HERE):
-        own = both(pv4, leaf_parent[b])
-        side = jnp.where(((leaf_octant[b] >> 1) & 1) == 1, own[1], own[0])
-        tiles.append(jnp.where((leaf_octant[b] >> 2) == 1, side[8:16], side[0:8]))
-    lw[...] = split_dot(jnp.concatenate(tiles, axis=0), leaf_table)
-    for b in range(LEAVES_HERE):
-        piece = lw[b * 8 : b * 8 + 8, :]
-        for t in range(2):
-            rows = pl.ds(t, 8, stride=2)
-            for i in range(2):
-                lv3[i, b, rows, :] = lv2[i, b, rows, :] + piece[:, i * 128 : i * 128 + 128]
+        put(pv4, slot, relaxed(h, beside, both(src, p)))
+
+    parent_final(0, first_parent)
+    parent_final(1, last_parent)
+
+    widen_leaves(pv4, leaf_slot, lv2, lv3)
     pack_faces(lv3, xs3, zb3)
     third = exchange(2, xs3, xr3, zb3)
     start_all(third)
     for k in range(3):
-        own = both(pv4, slot_parent[k])
-        for i in range(2):
-            parent_out[k, :, i * 128 : i * 128 + 128] = jnp.where(
-                slot_filled[k] == 1, own[i], 0.0
-            )
+        parent_final(2 + k, slot_parent[k])
+    column_sums(r >= middle)
+    plane_sums(r < middle)
     wait_arrivals(third)
     unpack_x(xr3)
     for b in range(LEAVES_HERE):
         h, beside = leaf_beside(lv3, zb3, b)
-        pair = relaxed(h, beside, lanes_of(rhs, b))
+        put(lv1, b, relaxed(h, beside, lanes_of(rhs, b)))
+    plane_sums(r >= middle)
+    mean_copy(0).wait_recv()
+    sums = msend[2] + mrecv[0]
+    mean = jnp.sum(sums) * (0.25 / (1024.0 * ranges))
+    for b in range(LEAVES_HERE):
         for i in range(2):
-            leaf_out[b, :, i * 128 : i * 128 + 128] = pair[i]
-
-    for copies in (first, second, third, halos, slabs):
+            leaf_out[b, :, i * 128 : i * 128 + 128] = lv1[i, b] - mean * le4[i, b]
+    for k in range(3):
+        own = both(pv4, 2 + k)
+        flat = both(pe4, slot_parent[k])
+        for i in range(2):
+            parent_out[k, :, i * 128 : i * 128 + 128] = jnp.where(
+                slot_filled[k] == 1, own[i] - mean * flat[i], 0.0
+            )
+
+    for copies in (first, second, third, fourth, halos, slabs):
         wait_departures(copies)
     for k in range(1, 16):
         octants(k).wait_send()
-    for k in range(16):
-        mean_copy(k).wait_send()
+    mean_copy(0).wait_send()
+    wait_departures(lower_sums)
+    wait_departures(upper_sums)
+    for k in order:
+        column_copy(k).wait_send()
 
 
 def local(rhs, leaf_neighbors, parent_neighbors, children, owners, parent_places):
     f32 = jnp.float32
     vmem = pl.BlockSpec(memory_space=pltpu.VMEM)
-    smem = pl.BlockSpec(memory_space=pltpu.SMEM)
-    kids = children.T
+    hbm = pl.BlockSpec(memory_space=pltpu.HBM)
     return pl.pallas_call(
         kernel,
         out_shape=(
             jax.ShapeDtypeStruct((8, 16, 256), f32),
             jax.ShapeDtypeStruct((3, 16, 256), f32),
         ),
-        in_specs=[vmem, smem, smem, smem, smem, smem, vmem],
+        in_specs=[hbm] * 6,
         out_specs=(vmem, vmem),
         scratch_shapes=[
+            pltpu.VMEM((8, 16, 256), f32),
+            pltpu.SMEM((8, 6), jnp.int32),
+            pltpu.SMEM((6, 512), jnp.int32),
+            pltpu.SMEM((8, 512), jnp.int32),
+            pltpu.SMEM((512,), jnp.int32),
+            pltpu.SMEM((512,), jnp.int32),
+            pltpu.VMEM((8, 512), jnp.int32),
+            pltpu.SemaphoreType.DMA((7,)),
+            pltpu.SMEM((96,), jnp.int32),
+            pltpu.VMEM((2, 17, 16, 128), f32),
+            pltpu.VMEM((2, 16, 16, 128), f32),
+            pltpu.VMEM((2, 9, 16, 128), f32),
+            pltpu.VMEM((2, 8, 16, 128), f32),
+            pltpu.VMEM((2, 8, 256), f32),
+            pltpu.VMEM((2, 8, 256), f32),
+            pltpu.VMEM((33, 1, 256), f32),
             pltpu.VMEM((2, 9, 16, 128), f32),
             pltpu.VMEM((2, 9, 16, 128), f32),
             pltpu.VMEM((2, 9, 16, 128), f32),
@@ -800,31 +1028,38 @@
             pltpu.VMEM((24, 256), f32),
             pltpu.VMEM((96, 256), f32),
             pltpu.VMEM((96, 256), f32),
-            pltpu.VMEM((2, 1, 128), f32),
+            pltpu.VMEM((3, 1, 128), f32),
+            pltpu.VMEM((31, 1, 128), f32),
             pltpu.VMEM((16, 1, 128), f32),
             pltpu.VMEM((64, 256), f32),
-            pltpu.SemaphoreType.DMA((3, 4)),
-            pltpu.SemaphoreType.DMA((3, 4)),
+            pltpu.SemaphoreType.DMA((4, 4)),
+            pltpu.SemaphoreType.DMA((4, 4)),
             pltpu.SemaphoreType.DMA((16,)),
             pltpu.SemaphoreType.DMA((16,)),
             pltpu.SemaphoreType.DMA((2,)),
             pltpu.SemaphoreType.DMA((2,)),
             pltpu.SemaphoreType.DMA((4,)),
             pltpu.SemaphoreType.DMA((4,)),
+            pltpu.SemaphoreType.DMA((31,)),
+            pltpu.SemaphoreType.DMA((31,)),
             pltpu.SemaphoreType.DMA((16,)),
             pltpu.SemaphoreType.DMA((16,)),
-            pltpu.SemaphoreType.REGULAR((3,)),
+            pltpu.SemaphoreType.REGULAR((6,)),
         ],
-        compiler_params=pltpu.CompilerParams(collective_id=0, has_side_effects=True),
+        compiler_params=pltpu.CompilerParams(collective_id=0, has_side_effects=True, vmem_limit_bytes=10 * 1024 * 1024),
         name="vcycle",
     )(
-        rhs,
-        leaf_neighbors,
-        parent_neighbors.T,
-        kids,
-        owners,
-        parent_places,
-        kids,
+        *(
+            pltpu.with_memory_space_constraint(v, pltpu.HBM)
+            for v in (
+                rhs,
+                leaf_neighbors,
+                parent_neighbors.T,
+                children.T,
+                owners,
+                parent_places,
+            )
+        )
     )
 
 

time: 47.4 us -> 40.2 us (0.85)
  Pallas kernels: 44.3 us -> 37.7 us
  local copies, waits for them, and re-layouts: 2.2 us -> 1.28 us
    pallas_call x1, Pallas kernels: 44.3 us -> 37.7 us  [local(): pl.pallas_call(kernel, out_shape=(jax.ShapeDtypeStruct((8, 16, 256), f32)...]
    unnamed x4 -> x2, local copies, waits for them, and re-layouts: 2.2 us -> 1.28 us
where the time goes in v2:
time: 40.2 us; the launch traced here: 39.6 us
  Pallas kernels  37.7 us (94%)
  local copies, waits for them, and re-layouts  1.28 us (3%)
  between operations  0.64 us (2%)
    pallas_call x1, Pallas kernels, local(): pl.pallas_call(kernel, out_shape=(jax.ShapeDtypeStruct((8, 16, 256), f32)...  37.7 us
    unnamed x2, local copies, waits for them, and re-layouts  1.28 us

profile of v2, /device:TPU:1, one launch (start us, length us, event | category | flops | bytes accessed | tf_op | source)
XLA Modules:
  0.0 39.6 jit_solution(13954547952330181226)
XLA Ops:
  0.6 37.7 %vcycle.1 = (f32[8,16,256]{2,1,0:T(8,128)S(1)}, f32[3,16,256]{2,1,0:T(8,128)S(1)}) custom-call(f32[8,16,256]{2,1,0:T(8,128)} %rhs_in.1, s32[8,6]{1,0:T(8,128)} %ln_in.1, s32[6,512]{1,0:T(8,128)} %bitcast.2, s32[8,512]{1,0:T(8,128)} %bitcast.3, s32[512]{0:T(512)} %ow_in.1, s32[512]{0:T(512)} %places_in.1), custom_call_target="tpu_custom_call" | custom-call | tf_op jit(solution)/shard_map/vcycle/pallas_call | solution.py:972
  38.4 0.7 %copy.10 = f32[8,16,256]{2,1,0:T(8,128)} copy(f32[8,16,256]{2,1,0:T(8,128)S(1)} %get-tuple-element.4) | data formatting | bytes 262144
  39.0 0.6 %copy.11 = f32[3,16,256]{2,1,0:T(8,128)} copy(f32[3,16,256]{2,1,0:T(8,128)S(1)} %get-tuple-element.5) | data formatting | bytes 98304

commit v3 on v2

--- a/solution.py
+++ b/solution.py
@@ -116,12 +116,14 @@
     lv1,
     lv2,
     lv3,
-    xs1,
-    xs2,
     xs3,
-    xr1,
-    xr2,
     xr3,
+    xsm,
+    xrm,
+    zsm,
+    zrm,
+    line_send,
+    lines,
     xt,
     zb1,
     zb2,
@@ -225,7 +227,24 @@
                 device_id_type=MESH,
             )
 
-    greetings = 4 + sum(exists(d).astype(jnp.int32) for d in (1, -1, 2, -2))
+    corners = tuple(
+        ((r + dz >= 0) & (r + dz < ranges) & (s + dx >= 0) & (s + dx < subs), dz, dx)
+        for dz in (-1, 1)
+        for dx in (-1, 1)
+    )
+    for there, dz, dx in corners:
+
+        @pl.when(there)
+        def _():
+            pl.semaphore_signal(
+                barrier,
+                inc=1,
+                device_id=((r + dz + ranges) % ranges, (s + dx + subs) % subs),
+                device_id_type=MESH,
+            )
+
+    greetings = 4 + sum(there.astype(jnp.int32) for there, _, _ in corners)
+    greetings = greetings + sum(exists(d).astype(jnp.int32) for d in (1, -1, 2, -2))
     greetings = greetings + sum(
         ((r - 2 * k >= 0) & (r - 2 * k < middle)).astype(jnp.int32) for k in range(2, 16)
     )
@@ -237,7 +256,7 @@
     zero_half = jnp.zeros((16, 128), jnp.float32)
     zeros = [zero_half, zero_half]
 
-    def pack_faces(values, xs, zb):
+    def pack_x(values, store):
         for h in range(2):
             low = jnp.zeros((8, 128), jnp.float32)
             high = jnp.zeros((8, 128), jnp.float32)
@@ -247,12 +266,21 @@
                     k = part * 8 + b
                     low = jnp.where(column8 == k, lane_roll(v, k), low)
                     high = jnp.where(column8 == k, lane_roll(v, k - 15), high)
-            xs[0, :, h * 128 : h * 128 + 128] = low
-            xs[1, :, h * 128 : h * 128 + 128] = high
+            store(0, h, low)
+            store(1, h, high)
+
+    def local_rows(values, zb):
         for b in range(LEAVES_HERE):
             put_row(zb, b, [values[i, b, 0:1, :] for i in range(2)])
             put_row(zb, 8 + b, [values[i, b, 15:16, :] for i in range(2)])
         zb[32] = jnp.zeros((1, 256), jnp.float32)
+
+    def pack_faces(values, xs, zb):
+        def store(side, h, value):
+            xs[side, :, h * 128 : h * 128 + 128] = value
+
+        pack_x(values, store)
+        local_rows(values, zb)
 
     def exchange(step, xs, xr, zb):
         def remote(source, target, slot, device):
@@ -301,17 +329,19 @@
             def _():
                 copy.wait_send()
 
-    def unpack_x(xr):
+    def unpack_faces(face_of):
         for h in range(2):
-            lanes = slice(h * 128, h * 128 + 128)
-            below = xr[0, :, lanes]
-            above = xr[1, :, lanes]
+            below = face_of(0, h)
+            above = face_of(1, h)
             for j in range(LEAVES_HERE):
                 for part in range(2):
                     k = part * 8 + j
                     rows = slice(part * 8, part * 8 + 8)
                     xt[0, h, j, rows, :] = lane_roll(below, -k)
                     xt[1, h, j, rows, :] = lane_roll(above, 15 - k)
+
+    def unpack_x(xr):
+        unpack_faces(lambda side, h: xr[side, :, h * 128 : h * 128 + 128])
 
     def leaf_beside(values, zb, b):
         h = both(values, b)
@@ -348,47 +378,6 @@
     for side in range(2):
         for ref in (hv, h2, own_rows):
             ref[side * 17 + 16] = jnp.zeros((1, 256), jnp.float32)
-
-    loads[0].wait()
-    for b in range(LEAVES_HERE):
-        put(lv1, b, [FACTOR * v for v in lanes_of(rhs, b)])
-    pack_faces(lv1, xs1, zb1)
-    pl.semaphore_wait(barrier, greetings)
-    first = exchange(0, xs1, xr1, zb1)
-    start_all(first)
-
-    def tell(stage):
-        distance = 2 << stage
-
-        @pl.when((r >= middle) & (r + distance < ranges))
-        def _():
-            pl.semaphore_signal(
-                tok.at[stage],
-                inc=1,
-                device_id=((r + distance) % ranges, s),
-                device_id_type=MESH,
-            )
-
-        @pl.when(r - distance >= middle)
-        def _():
-            pl.semaphore_signal(
-                tok.at[stage],
-                inc=1,
-                device_id=((r - distance + ranges) % ranges, s),
-                device_id_type=MESH,
-            )
-
-    def hear(stage):
-        distance = 2 << stage
-        peers = ((r >= middle) & (r + distance < ranges)).astype(jnp.int32)
-        peers = peers + (r - distance >= middle).astype(jnp.int32)
-
-        @pl.when(peers > 0)
-        def _():
-            pl.semaphore_wait(tok.at[stage], peers)
-
-    tell(0)
-    signal_sub(tok.at[4], (1, -1, 4, -4))
 
     loads[1].wait()
     here = r * subs + s
@@ -410,6 +399,130 @@
                     n >= 0, (n & 7) + jnp.where(remote, far_base, own_base), 32
                 )
 
+    leaf_near = []
+    leaf_far = []
+    for b in range(LEAVES_HERE):
+        far = [leaf_z[b][f] >= 16 for f in range(2)]
+        leaf_near.append([jnp.where(far[f], 32, leaf_z[b][f]) for f in range(2)])
+        leaf_far.append([jnp.where(far[f], leaf_z[b][f], 32) for f in range(2)])
+    loads[0].wait()
+    for b in range(LEAVES_HERE):
+        put(lv1, b, [FACTOR * v for v in lanes_of(rhs, b)])
+    local_rows(lv1, zb1)
+    for b in range(LEAVES_HERE):
+        h = both(lv1, b)
+        xsum = x_sum(lane, h, [0.0, 0.0], [0.0, 0.0])
+        ysum = y_sum(lane, h, lv1[1, leaf_y[b][0]], lv1[0, leaf_y[b][1]])
+        zsum = z_sum(row, h, row_pair(zb1, leaf_near[b][0]), row_pair(zb1, leaf_near[b][1]))
+        beside = [xsum[i] + ysum[i] + zsum[i] for i in range(2)]
+        put(res, b, relaxed(h, beside, lanes_of(rhs, b)))
+    row8 = row[0:8]
+    for field, values in ((0, lv1), (1, res)):
+
+        def store(side, h, value):
+            xsm[side, field, :, h * 128 : h * 128 + 128] = value
+
+        pack_x(values, store)
+        for b in range(LEAVES_HERE):
+            for i in range(2):
+                lanes = slice(i * 128, i * 128 + 128)
+                zsm[0, field, b : b + 1, lanes] = values[i, b, 0:1, :]
+                zsm[1, field, b : b + 1, lanes] = values[i, b, 15:16, :]
+    x_lines = jnp.full((8, 128), -100.0, jnp.float32)
+    z_lines = jnp.full((8, 128), -100.0, jnp.float32)
+    for b in range(LEAVES_HERE):
+        down = jnp.where(leaf_z[b][0] >= 16, leaf_z[b][0] - 8, -100).astype(jnp.float32)
+        up = jnp.where(leaf_far[b][1] < 32, leaf_z[b][1] - 24, -100).astype(jnp.float32)
+        down = jnp.where(leaf_z[b][0] < 32, down, -100.0)
+        x_lines = jnp.where((row8 == 0) & (column8 == b), down, x_lines)
+        x_lines = jnp.where((row8 == 7) & (column8 == 8 + b), up, x_lines)
+        left = jnp.where(leaf_x[b][0] < 8, leaf_x[b][0], -100).astype(jnp.float32)
+        right = jnp.where(leaf_x[b][1] < 8, leaf_x[b][1], -100).astype(jnp.float32)
+        z_lines = jnp.where((row8 == b) & (column8 == 0), left, z_lines)
+        z_lines = jnp.where((row8 == b) & (column8 == 15), right, z_lines)
+    for side in range(2):
+        for i in range(2):
+            lanes = slice(i * 128, i * 128 + 128)
+            xsm[side, 2, :, lanes] = x_lines
+            zsm[side, 2, :, lanes] = z_lines
+            for zi in range(2):
+                at = 0 if zi == 0 else 7
+                line_send[2 * zi + side, :, lanes] = xsm[side, 0, at : at + 1, lanes]
+
+    def first_copy(step, slot, source, target, device):
+        return pltpu.make_async_remote_copy(
+            src_ref=source,
+            dst_ref=target,
+            send_sem=a_send.at[step, slot],
+            recv_sem=a_recv.at[step, slot],
+            device_id=device,
+            device_id_type=MESH,
+        )
+
+    pl.semaphore_wait(barrier, greetings)
+    first = (
+        (
+            s > 0,
+            s < subs - 1,
+            first_copy(0, 0, xsm.at[0], xrm.at[1], (r, (s + subs - 1) % subs)),
+        ),
+        (s < subs - 1, s > 0, first_copy(0, 1, xsm.at[1], xrm.at[0], (r, (s + 1) % subs))),
+        (
+            r > 0,
+            r < ranges - 1,
+            first_copy(0, 2, zsm.at[0], zrm.at[1], ((r + ranges - 1) % ranges, s)),
+        ),
+        (r < ranges - 1, r > 0, first_copy(0, 3, zsm.at[1], zrm.at[0], ((r + 1) % ranges, s))),
+    )
+    first = first + tuple(
+        (
+            there,
+            corners[3 - k][0],
+            first_copy(
+                1,
+                k,
+                line_send.at[k],
+                lines.at[3 - k],
+                ((r + dz + ranges) % ranges, (s + dx + subs) % subs),
+            ),
+        )
+        for k, (there, dz, dx) in enumerate(corners)
+    )
+    start_all(first)
+
+    def tell(stage):
+        distance = 2 << stage
+
+        @pl.when((r >= middle) & (r + distance < ranges))
+        def _():
+            pl.semaphore_signal(
+                tok.at[stage],
+                inc=1,
+                device_id=((r + distance) % ranges, s),
+                device_id_type=MESH,
+            )
+
+        @pl.when(r - distance >= middle)
+        def _():
+            pl.semaphore_signal(
+                tok.at[stage],
+                inc=1,
+                device_id=((r - distance + ranges) % ranges, s),
+                device_id_type=MESH,
+            )
+
+    def hear(stage):
+        distance = 2 << stage
+        peers = ((r >= middle) & (r + distance < ranges)).astype(jnp.int32)
+        peers = peers + (r - distance >= middle).astype(jnp.int32)
+
+        @pl.when(peers > 0)
+        def _():
+            pl.semaphore_wait(tok.at[stage], peers)
+
+    tell(0)
+    signal_sub(tok.at[4], (1, -1, 4, -4))
+
     def numbers(shape, dim):
         return lax.broadcasted_iota(jnp.int32, shape, dim)
 
@@ -421,16 +534,6 @@
     restrict = table(
         ((source_id % 256) // 32 == target_id // 16)
         & ((source_id % 16) // 2 + (source_id // 256) * 8 == target_id % 16)
-    )
-    fine = numbers((256, 256), 0)
-    grid = numbers((256, 256), 1)
-    coarse_table = table(
-        (fine // 64 == (grid // 32) % 4) & ((fine % 16) // 4 == grid % 4)
-    )
-    grid_in = numbers((256, 256), 0)
-    fine_out = numbers((256, 256), 1)
-    widen_table = table(
-        (fine_out // 64 == (grid_in // 32) % 4) & ((fine_out % 16) // 4 == grid_in % 4)
     )
     octant_in = numbers((128, 256), 0)
     leaf_cell = numbers((128, 256), 1)
@@ -470,20 +573,6 @@
         for side in range(2)
     ]
 
-    hear(0)
-    tell(1)
-    wait_arrivals(first)
-    hear(1)
-    tell(2)
-    pl.semaphore_wait(tok.at[4], 4)
-    signal_sub(tok.at[5], (2, -2))
-    unpack_x(xr1)
-    for b in range(LEAVES_HERE):
-        h, beside = leaf_beside(lv1, zb1, b)
-        put(lv2, b, relaxed(h, beside, lanes_of(rhs, b)))
-    pack_faces(lv2, xs2, zb2)
-    second = exchange(1, xs2, xr2, zb2)
-    start_all(second)
 
     def missing(base, p, f):
         return jnp.where(pn[f, base + p] < 0, FACTOR, 0.0).astype(jnp.float32)
@@ -568,11 +657,74 @@
 
     widen_leaves(geo, leaf_parent, None, lv3)
 
-    wait_arrivals(second)
-    unpack_x(xr2)
+    hear(0)
+    tell(1)
+    pl.semaphore_wait(tok.at[4], 4)
+    signal_sub(tok.at[5], (2, -2))
+    wait_arrivals(first)
+    hear(1)
+    tell(2)
+    unpack_faces(lambda side, h: xrm[side, 0, :, h * 128 : h * 128 + 128])
+    for side in range(2):
+        for n in range(LEAVES_HERE):
+            zb1[16 + 8 * side + n] = zrm[side, 0, n : n + 1, :]
     for b in range(LEAVES_HERE):
-        h, beside = leaf_beside(lv2, zb2, b)
-        put(res, b, rest(h, beside, lanes_of(rhs, b)))
+        low = [xt[0, i, leaf_x[b][0]] for i in range(2)]
+        high = [xt[1, i, leaf_x[b][1]] for i in range(2)]
+        below = row_pair(zb1, leaf_far[b][0])
+        above = row_pair(zb1, leaf_far[b][1])
+        pair = []
+        for i in range(2):
+            more = jnp.where(column == 0, low[i], 0.0) + jnp.where(column == 15, high[i], 0.0)
+            more = more + jnp.where(row == 0, below[i], 0.0) + jnp.where(row == 15, above[i], 0.0)
+            pair.append(res[i, b] + FACTOR * more)
+        put(lv2, b, pair)
+    local_rows(lv2, zb2)
+
+    def x_face(side, h):
+        lanes = slice(h * 128, h * 128 + 128)
+        hit = xrm[side, 2, :, lanes] - column8.astype(jnp.float32)
+        more = jnp.zeros((8, 128), jnp.float32)
+        for zi in range(2):
+            line = jnp.broadcast_to(lines[2 * zi + side, :, lanes], (8, 128))
+            for d in range(1, 16):
+                shift = d if zi == 0 else -d
+                wanted = (row8 == (0 if zi == 0 else 7)) & (hit == shift)
+                more = jnp.where(wanted, lane_roll(line, -shift), more)
+        return xrm[side, 1, :, lanes] + FACTOR * more
+
+    unpack_faces(x_face)
+    for zi in range(2):
+        for h in range(2):
+            lanes = slice(h * 128, h * 128 + 128)
+            wanted = zrm[zi, 2, :, lanes]
+            left = jnp.broadcast_to(lines[2 * zi, :, lanes], (8, 128))
+            right = jnp.broadcast_to(lines[2 * zi + 1, :, lanes], (8, 128))
+            more = jnp.zeros((8, 128), jnp.float32)
+            for k in range(8):
+                at = k + 8 if zi == 0 else k
+                moved = jnp.where(column8 == 0, lane_roll(left, -at), lane_roll(right, 15 - at))
+                more = jnp.where(wanted == k, moved, more)
+            rows_tmp[zi * 8 : zi * 8 + 8, lanes] = zrm[zi, 1, :, lanes] + FACTOR * more
+    for n in range(16):
+        zb2[16 + n] = rows_tmp[n : n + 1, :]
+    for b in range(LEAVES_HERE):
+        v = both(lv1, b)
+        h = both(lv2, b)
+        side_gain = [jnp.where(leaf_x[b][f] < 8, FACTOR, 0.0).astype(jnp.float32) for f in range(2)]
+        far_gain = [
+            jnp.where(leaf_far[b][f] < 32, FACTOR, 0.0).astype(jnp.float32) for f in range(2)
+        ]
+        low = [xt[0, i, leaf_x[b][0]] + side_gain[0] * v[i] for i in range(2)]
+        high = [xt[1, i, leaf_x[b][1]] + side_gain[1] * v[i] for i in range(2)]
+        below = row_pair(zb2, leaf_z[b][0])
+        above = row_pair(zb2, leaf_z[b][1])
+        below = [below[i] + far_gain[0] * v[i][0:1] for i in range(2)]
+        above = [above[i] + far_gain[1] * v[i][15:16] for i in range(2)]
+        xsum = x_sum(lane, h, low, high)
+        ysum = y_sum(lane, h, lv2[1, leaf_y[b][0]], lv2[0, leaf_y[b][1]])
+        zsum = z_sum(row, h, below, above)
+        put(res, b, rest(h, [xsum[i] + ysum[i] + zsum[i] for i in range(2)], lanes_of(rhs, b)))
     pieces = []
     for b in range(LEAVES_HERE):
         pieces.append(
@@ -600,7 +752,6 @@
         )
 
     order = (8, 2, 10, 6, 14, 7, 9, 5, 11, 3, 13, 4, 12, 1, 15)
-    hear(2)
     pl.semaphore_wait(tok.at[5], 2)
     for k in order:
         octants(k).start()
@@ -629,12 +780,23 @@
         v = both(res, b)
         total = total + q[0] * v[0] + q[1] * v[1]
     msend[0] = 0.5 * jnp.sum(total, axis=0, keepdims=True)
+    hear(2)
     start_all(lower_sums)
 
     @pl.when(r >= middle)
     def _():
         start_all(upper_sums)
 
+    fine = numbers((256, 256), 0)
+    grid = numbers((256, 256), 1)
+    coarse_table = table(
+        (fine // 64 == (grid // 32) % 4) & ((fine % 16) // 4 == grid % 4)
+    )
+    grid_in = numbers((256, 256), 0)
+    fine_out = numbers((256, 256), 1)
+    widen_table = table(
+        (fine_out // 64 == (grid_in // 32) % 4) & ((fine_out % 16) // 4 == grid_in % 4)
+    )
     slot_parent = [jnp.int32(0)] * 3
     slot_filled = [jnp.int32(0)] * 3
     seen = jnp.int32(0)
@@ -954,7 +1116,7 @@
                 slot_filled[k] == 1, own[i] - mean * flat[i], 0.0
             )
 
-    for copies in (first, second, third, fourth, halos, slabs):
+    for copies in (first, third, fourth, halos, slabs):
         wait_departures(copies)
     for k in range(1, 16):
         octants(k).wait_send()
@@ -999,10 +1161,12 @@
             pltpu.VMEM((2, 9, 16, 128), f32),
             pltpu.VMEM((2, 8, 256), f32),
             pltpu.VMEM((2, 8, 256), f32),
-            pltpu.VMEM((2, 8, 256), f32),
-            pltpu.VMEM((2, 8, 256), f32),
-            pltpu.VMEM((2, 8, 256), f32),
-            pltpu.VMEM((2, 8, 256), f32),
+            pltpu.VMEM((2, 3, 8, 256), f32),
+            pltpu.VMEM((2, 3, 8, 256), f32),
+            pltpu.VMEM((2, 3, 8, 256), f32),
+            pltpu.VMEM((2, 3, 8, 256), f32),
+            pltpu.VMEM((4, 1, 256), f32),
+            pltpu.VMEM((4, 1, 256), f32),
             pltpu.VMEM((2, 2, 9, 16, 128), f32),
             pltpu.VMEM((33, 1, 256), f32),
             pltpu.VMEM((33, 1, 256), f32),

time: 40.2 us -> 40.7 us (1.012)
  Pallas kernels: 37.7 us -> 38.3 us
    pallas_call x1, Pallas kernels: 37.7 us -> 38.3 us  [local(): pl.pallas_call(kernel, out_shape=(jax.ShapeDtypeStruct((8, 16, 256), f32)...]
where the time goes in v3:
time: 40.7 us; the launch traced here: 40.2 us
  Pallas kernels  38.3 us (94%)
  local copies, waits for them, and re-layouts  1.28 us (3%)
  between operations  0.64 us (2%)
    pallas_call x1, Pallas kernels, local(): pl.pallas_call(kernel, out_shape=(jax.ShapeDtypeStruct((8, 16, 256), f32)...  38.3 us
    unnamed x2, local copies, waits for them, and re-layouts  1.28 us

profile of v3, /device:TPU:1, one launch (start us, length us, event | category | flops | bytes accessed | tf_op | source)
XLA Modules:
  0.0 40.2 jit_solution(10405720850693918680)
XLA Ops:
  0.6 38.3 %vcycle.1 = (f32[8,16,256]{2,1,0:T(8,128)S(1)}, f32[3,16,256]{2,1,0:T(8,128)S(1)}) custom-call(f32[8,16,256]{2,1,0:T(8,128)} %rhs_in.1, s32[8,6]{1,0:T(8,128)} %ln_in.1, s32[6,512]{1,0:T(8,128)} %bitcast.2, s32[8,512]{1,0:T(8,128)} %bitcast.3, s32[512]{0:T(512)} %ow_in.1, s32[512]{0:T(512)} %places_in.1), custom_call_target="tpu_custom_call" | custom-call | tf_op jit(solution)/shard_map/vcycle/pallas_call | solution.py:1134
  38.9 0.7 %copy.10 = f32[8,16,256]{2,1,0:T(8,128)} copy(f32[8,16,256]{2,1,0:T(8,128)S(1)} %get-tuple-element.4) | data formatting | bytes 262144
  39.6 0.6 %copy.11 = f32[3,16,256]{2,1,0:T(8,128)} copy(f32[3,16,256]{2,1,0:T(8,128)S(1)} %get-tuple-element.5) | data formatting | bytes 98304

commit v4 on v3

--- a/solution.py
+++ b/solution.py
@@ -574,6 +574,9 @@
     ]
 
 
+    hear(0)
+    tell(1)
+
     def missing(base, p, f):
         return jnp.where(pn[f, base + p] < 0, FACTOR, 0.0).astype(jnp.float32)
 
@@ -657,13 +660,11 @@
 
     widen_leaves(geo, leaf_parent, None, lv3)
 
-    hear(0)
-    tell(1)
+    hear(1)
+    tell(2)
     pl.semaphore_wait(tok.at[4], 4)
     signal_sub(tok.at[5], (2, -2))
     wait_arrivals(first)
-    hear(1)
-    tell(2)
     unpack_faces(lambda side, h: xrm[side, 0, :, h * 128 : h * 128 + 128])
     for side in range(2):
         for n in range(LEAVES_HERE):
@@ -780,8 +781,13 @@
         v = both(res, b)
         total = total + q[0] * v[0] + q[1] * v[1]
     msend[0] = 0.5 * jnp.sum(total, axis=0, keepdims=True)
+    start_all(
+        tuple((sends & (r - 2 * k < middle), None, c) for k, (sends, _, c) in enumerate(lower_sums, 1))
+    )
     hear(2)
-    start_all(lower_sums)
+    start_all(
+        tuple((sends & (r - 2 * k >= middle), None, c) for k, (sends, _, c) in enumerate(lower_sums, 1))
+    )
 
     @pl.when(r >= middle)
     def _():

time: 40.7 us -> 39 us (0.958)
  Pallas kernels: 38.3 us -> 36.6 us
    pallas_call x1, Pallas kernels: 38.3 us -> 36.6 us  [local(): pl.pallas_call(kernel, out_shape=(jax.ShapeDtypeStruct((8, 16, 256), f32)...]
where the time goes in v4:
time: 39 us; the launch traced here: 38.5 us
  Pallas kernels  36.6 us (94%)
  local copies, waits for them, and re-layouts  1.28 us (3%)
  between operations  0.64 us (2%)
    pallas_call x1, Pallas kernels, local(): pl.pallas_call(kernel, out_shape=(jax.ShapeDtypeStruct((8, 16, 256), f32)...  36.6 us
    unnamed x2, local copies, waits for them, and re-layouts  1.28 us

profile of v4, /device:TPU:1, one launch (start us, length us, event | category | flops | bytes accessed | tf_op | source)
XLA Modules:
  0.0 38.5 jit_solution(11536432824640820712)
XLA Ops:
  0.6 36.6 %vcycle.1 = (f32[8,16,256]{2,1,0:T(8,128)S(1)}, f32[3,16,256]{2,1,0:T(8,128)S(1)}) custom-call(f32[8,16,256]{2,1,0:T(8,128)} %rhs_in.1, s32[8,6]{1,0:T(8,128)} %ln_in.1, s32[6,512]{1,0:T(8,128)} %bitcast.2, s32[8,512]{1,0:T(8,128)} %bitcast.3, s32[512]{0:T(512)} %ow_in.1, s32[512]{0:T(512)} %places_in.1), custom_call_target="tpu_custom_call" | custom-call | tf_op jit(solution)/shard_map/vcycle/pallas_call | solution.py:1140
  37.2 0.7 %copy.10 = f32[8,16,256]{2,1,0:T(8,128)} copy(f32[8,16,256]{2,1,0:T(8,128)S(1)} %get-tuple-element.4) | data formatting | bytes 262144
  37.9 0.6 %copy.11 = f32[3,16,256]{2,1,0:T(8,128)} copy(f32[3,16,256]{2,1,0:T(8,128)S(1)} %get-tuple-element.5) | data formatting | bytes 98304

commit v5 on v4

--- a/solution.py
+++ b/solution.py
@@ -607,12 +607,10 @@
         high = [lane_roll(v, 15) for v in both(values, g[1])]
         xsum = x_sum(lane, h, low, high)
         ysum = y_sum(lane, h, values[1, g[2]], values[0, g[3]])
-        zsum = z_sum(
-            row,
-            h,
-            row_pair(halo, g[4]),
-            row_pair(halo, g[5] + 17),
-        )
+        if halo is None:
+            zsum = z_sum(row, h, [0.0, 0.0], [0.0, 0.0])
+        else:
+            zsum = z_sum(row, h, row_pair(halo, g[4]), row_pair(halo, g[5] + 17))
         return h, [xsum[i] + ysum[i] + zsum[i] for i in range(2)]
 
     for p in range(PARENTS_HERE):
@@ -992,6 +990,13 @@
     for p in range(PARENTS_HERE):
         put(pv1, p, [FACTOR * v for v in both(src, p)])
 
+    for p in range(PARENTS_HERE):
+        put_row(own_rows, p, [pv1[i, p, 0:1, :] for i in range(2)])
+        put_row(own_rows, 17 + p, [pv1[i, p, 15:16, :] for i in range(2)])
+    for p in range(PARENTS_HERE):
+        h, beside = parent_beside(pv1, None, p)
+        put(pv2, p, relaxed(h, beside, both(src, p)))
+
     wait_arrivals(halos)
 
     def gather(ref, index_of):
@@ -1001,9 +1006,6 @@
 
     for side in range(2):
         spread(hv, side, [FACTOR * hrecv[side, 0, :, i * 128 : i * 128 + 128] for i in range(2)])
-    for p in range(PARENTS_HERE):
-        put_row(own_rows, p, [pv1[i, p, 0:1, :] for i in range(2)])
-        put_row(own_rows, 17 + p, [pv1[i, p, 15:16, :] for i in range(2)])
     for side in range(2):
         near = [hrecv[side, 0, :, i * 128 : i * 128 + 128] for i in range(2)]
         deep = [hrecv[side, 1, :, i * 128 : i * 128 + 128] for i in range(2)]
@@ -1021,8 +1023,12 @@
         spread(h2, side, flat_pair(halo_two, slice(side * 16, side * 16 + 16)))
 
     for p in range(PARENTS_HERE):
-        h, beside = parent_beside(pv1, hv, p)
-        put(pv2, p, relaxed(h, beside, both(src, p)))
+        g = own_ghost[p]
+        below = row_pair(hv, g[4])
+        above = row_pair(hv, g[5] + 17)
+        for i in range(2):
+            pv2[i, p, 0:1, :] = pv2[i, p, 0:1, :] + FACTOR * below[i]
+            pv2[i, p, 15:16, :] = pv2[i, p, 15:16, :] + FACTOR * above[i]
     for p in range(PARENTS_HERE):
         h, beside = parent_beside(pv2, h2, p)
         put(pv4, p, rest(h, beside, both(src, p)))

time: 39 us -> 39 us (level)
  no operation moved by 1% of the time
where the time goes in v5:
time: 39 us; the launch traced here: 38.5 us
  Pallas kernels  36.6 us (94%)
  local copies, waits for them, and re-layouts  1.28 us (3%)
  between operations  0.64 us (2%)
    pallas_call x1, Pallas kernels, local(): pl.pallas_call(kernel, out_shape=(jax.ShapeDtypeStruct((8, 16, 256), f32)...  36.6 us
    unnamed x2, local copies, waits for them, and re-layouts  1.28 us

profile of v5, /device:TPU:1, one launch (start us, length us, event | category | flops | bytes accessed | tf_op | source)
XLA Modules:
  0.0 38.5 jit_solution(17243414923599281079)
XLA Ops:
  0.6 36.6 %vcycle.1 = (f32[8,16,256]{2,1,0:T(8,128)S(1)}, f32[3,16,256]{2,1,0:T(8,128)S(1)}) custom-call(f32[8,16,256]{2,1,0:T(8,128)} %rhs_in.1, s32[8,6]{1,0:T(8,128)} %ln_in.1, s32[6,512]{1,0:T(8,128)} %bitcast.2, s32[8,512]{1,0:T(8,128)} %bitcast.3, s32[512]{0:T(512)} %ow_in.1, s32[512]{0:T(512)} %places_in.1), custom_call_target="tpu_custom_call" | custom-call | tf_op jit(solution)/shard_map/vcycle/pallas_call | solution.py:1146
  37.2 0.7 %copy.10 = f32[8,16,256]{2,1,0:T(8,128)} copy(f32[8,16,256]{2,1,0:T(8,128)S(1)} %get-tuple-element.4) | data formatting | bytes 262144
  37.9 0.6 %copy.11 = f32[3,16,256]{2,1,0:T(8,128)} copy(f32[3,16,256]{2,1,0:T(8,128)S(1)} %get-tuple-element.5) | data formatting | bytes 98304
